TPU v7x, 128 devices: a whole 4x4x4 slice. The times are simulated.
128 devices in a mesh: batch: 1, col: 2 (over core), row: 64 (over z, y, x).
Axes of the slice: x: 4, y: 4, z: 4, core: 2. Of those that a mesh axis runs over, the one named last changes fastest.
Arguments:
- x: bfloat16 [16, 512, 128, 256], P('batch', 'row', 'col')
- w_down_1: bfloat16 [3, 3, 256, 512], replicated
- b_down_1: float32 [512], replicated
- w_conv_1: bfloat16 [3, 3, 512, 512], replicated
- b_conv_1: float32 [512], replicated
- w_proj_1: bfloat16 [256, 512], replicated
- w_down_2: bfloat16 [3, 3, 512, 1024], replicated
- b_down_2: float32 [1024], replicated
- w_conv_2: bfloat16 [3, 3, 1024, 1024], replicated
- b_conv_2: float32 [1024], replicated
- w_proj_2: bfloat16 [512, 1024], replicated
- w_down_3: bfloat16 [3, 3, 1024, 2048], replicated
- b_down_3: float32 [2048], replicated
- w_conv_3: bfloat16 [3, 3, 2048, 2048], replicated
- b_conv_3: float32 [2048], replicated
- w_proj_3: bfloat16 [1024, 2048], replicated
Outputs:
- output: bfloat16 [16, 64, 16, 2048], P('batch', 'row', 'col')
All inputs are finite; a program needn't handle non-finite values.
Results may differ from a plain program's by a relative error of at most 0.00593535.
Values are sent between devices in bfloat16 or wider.
A program may use at most 1 GiB of HBM per device.

v0:
```python
import jax
import jax.numpy as jnp
from jax import lax
from jax.sharding import PartitionSpec as P

CONV_DIMS = ("NHWC", "HWIO", "NHWC")


def from_lower(edge_part, axis_name, dev_count):
    return lax.ppermute(edge_part, axis_name, [(dev_index, dev_index + 1) for dev_index in range(dev_count - 1)])


def from_upper(edge_part, axis_name, dev_count):
    return lax.ppermute(edge_part, axis_name, [(dev_index + 1, dev_index) for dev_index in range(dev_count - 1)])


def pad_lower(tile_in, row_count, col_count):
    top_row = from_lower(tile_in[:, -1:], "row", row_count)
    tall_tile = jnp.concatenate([top_row, tile_in], axis=1)
    left_col = from_lower(tall_tile[:, :, -1:], "col", col_count)
    return jnp.concatenate([left_col, tall_tile], axis=2)


def pad_both(tile_in, row_count, col_count):
    top_row = from_lower(tile_in[:, -1:], "row", row_count)
    bottom_row = from_upper(tile_in[:, :1], "row", row_count)
    tall_tile = jnp.concatenate([top_row, tile_in, bottom_row], axis=1)
    left_col = from_lower(tall_tile[:, :, -1:], "col", col_count)
    right_col = from_upper(tall_tile[:, :, :1], "col", col_count)
    return jnp.concatenate([left_col, tall_tile, right_col], axis=2)


def conv_valid(act_in, weight, stride):
    return lax.conv_general_dilated(act_in, weight, (stride, stride), "VALID", dimension_numbers=CONV_DIMS, preferred_element_type=jnp.float32)


def basic_block(z_prev, w_down, b_down, w_conv, b_conv, w_proj, row_count, col_count):
    y_act = jax.nn.relu(conv_valid(pad_lower(z_prev, row_count, col_count), w_down, 2) + b_down).astype(jnp.bfloat16)
    shortcut = jnp.einsum("bhwc,cd->bhwd", z_prev[:, ::2, ::2], w_proj, preferred_element_type=jnp.float32)
    z_next = jax.nn.relu(conv_valid(pad_both(y_act, row_count, col_count), w_conv, 1) + shortcut + b_conv)
    return z_next.astype(jnp.bfloat16)


def solution(mesh):
    row_count = mesh.shape["row"]
    col_count = mesh.shape["col"]
    tile_spec = P("batch", "row", "col")

    def local_blocks(x_tile, *params):
        act_out = x_tile
        for stage in range(3):
            stage_params = params[5 * stage:5 * stage + 5]
            act_out = basic_block(act_out, stage_params[0], stage_params[1], stage_params[2], stage_params[3], stage_params[4], row_count, col_count)
        return act_out

    return jax.shard_map(local_blocks, mesh=mesh, in_specs=(tile_spec,) + (P(),) * 15, out_specs=tile_spec, check_vma=False)
```

profile of v0, /device:TPU:97, one launch (start us, length us, event | category | flops | bytes accessed | tf_op | source)
XLA Modules:
  0.0 253.7 jit_solution(1459704128754796118)
XLA Ops:
  1.5 3.1 %collective-permute-start = (bf16[16,1,64,256]{3,0,2,1:T(8,128)(2,1)S(1)}, bf16[16,1,64,256]{3,0,2,1:T(8,128)(2,1)S(1)}, u32[]{:S(2)}, u32[]{:S(2)}) collective-permute-start(bf16[16,1,64,256]{3,0,2,1:T(8,128)(2,1)S(1)} %copy.36), channel_id=1, source_target_pairs={{0,1},{1,2},{2,3},{3,4},{4,5},{5,6},{6,7},{7,8},{8,9},{9,10},{10,1... | collective-permute-start | bytes 1572872 | tf_op jit(solution)/shard_map/ppermute | solution.py:10
  4.7 15.8 %collective-permute-done = bf16[16,1,64,256]{3,0,2,1:T(8,128)(2,1)S(1)} collective-permute-done((bf16[16,1,64,256]{3,0,2,1:T(8,128)(2,1)S(1)}, bf16[16,1,64,256]{3,0,2,1:T(8,128)(2,1)S(1)}, u32[]{:S(2)}, u32[]{:S(2)}) %collective-permute-start) | collective-permute-done | bytes 524320 | tf_op jit(solution)/shard_map/ppermute | solution.py:10
  20.5 4.8 %constant_dynamic-update-slice_fusion = bf16[16,9,64,256]{3,0,2,1:T(8,128)(2,1)S(1)} fusion(bf16[16,9,64,256]{3,0,2,1:T(8,128)(2,1)S(1)} %constant_dynamic-update-slice_fusion.1, bf16[16,8,64,256]{3,2,1,0:T(8,128)(2,1)} %param.16), kind=kLoop, calls=%fused_computation.77 | loop fusion | bytes 8388608 | tf_op jit(solution)/shard_map/concatenate | solution.py:19
  26.6 2.8 %collective-permute-done.1 = bf16[16,9,1,256]{3,0,2,1:T(8,128)(2,1)S(1)} collective-permute-done((bf16[16,9,1,256]{3,0,2,1:T(8,128)(2,1)S(1)}, bf16[16,9,1,256]{3,0,2,1:T(8,128)(2,1)S(1)}, u32[]{:S(2)}, u32[]{:S(2)}) %collective-permute-start.1) | collective-permute-done | bytes 73760 | tf_op jit(solution)/shard_map/ppermute | solution.py:10
  29.4 5.2 %maximum_convert_fusion.1 = bf16[16,4,32,512]{3,0,2,1:T(8,128)(2,1)S(1)} fusion(f32[512]{0:T(512)S(1)} %copy-done.12, bf16[3,3,256,512]{3,2,1,0:T(8,128)(2,1)S(1)} %copy-done, bf16[16,9,64,256]{3,0,2,1:T(8,128)(2,1)S(1)} %constant_dynamic-update-slice_fusion, bf16[16,9,1,256]{3,0,2,1:T(8,128)(2,1)S(1)} %collective-permute-done.1), kind=kOutput, calls=%fused_computation.7 | convolution fusion | flops 4837380096 | bytes 9250816 | tf_op jit(solution)/shard_map/conv_general_dilated | solution.py:34
  34.6 1.3 copy-done.3
  36.9 2.0 collective-permute-start.2
  39.0 7.6 %collective-permute-start.3 = (bf16[16,1,32,512]{3,0,2,1:T(8,128)(2,1)}, bf16[16,1,32,512]{3,0,2,1:T(8,128)(2,1)}, u32[]{:S(2)}, u32[]{:S(2)}) collective-permute-start(bf16[16,1,32,512]{3,0,2,1:T(8,128)(2,1)} %get-tuple-element.10), channel_id=1, source_target_pairs={{1,0},{2,1},{3,2},{4,3},{5,4},{6,5},{7,6},{8,7},{9,8},{10,9},{11,1... | collective-permute-start | bytes 1572872 | tf_op jit(solution)/shard_map/ppermute | solution.py:14
  46.6 27.8 %slice.64 = bf16[16,4,32,256]{3,2,1,0:T(8,128)(2,1)S(1)} slice(bf16[16,8,64,256]{3,2,1,0:T(8,128)(2,1)} %param.16), slice={[0:16:1], [0:8:2], [0:64:2], [0:256:1]} | slice | bytes 2097152 | tf_op jit(solution)/shard_map/slice | solution.py:39
  75.3 1.4 collective-permute-start.4
  76.7 3.0 %collective-permute-start.5 = (bf16[16,6,1,512]{3,0,2,1:T(8,128)(2,1)S(1)}, bf16[16,6,1,512]{3,0,2,1:T(8,128)(2,1)S(1)}, u32[]{:S(2)}, u32[]{:S(2)}) collective-permute-start(bf16[16,6,1,512]{3,0,2,1:T(8,128)(2,1)S(1)} %get-tuple-element.6), channel_id=1, source_target_pairs={{64,0},{65,1},{66,2},{67,3},{68,4},{69,5},{70,6},{71,7},{72,8},{73... | collective-permute-start | bytes 294920 | tf_op jit(solution)/shard_map/ppermute | solution.py:14
  80.7 13.2 %maximum_convert_fusion = bf16[16,4,32,512]{3,0,2,1:T(8,128)(2,1)S(1)} fusion(f32[16,4,32,512]{3,0,2,1:T(8,128)S(1)} %fusion.64, bf16[3,3,512,512]{3,2,1,0:T(8,128)(2,1)} %param.19, bf16[16,6,1,512]{3,0,2,1:T(8,128)(2,1)S(1)} %collective-permute-done.5, bf16[16,1,32,512]{3,0,2,1:T(8,128)(2,1)} %collective-permute-done.3, ...), kind=kOutput, calls=%fused_computation.6 | convolution fusion | flops 9674555392 | bytes 14354432 | tf_op jit(solution)/shard_map/conv_general_dilated | solution.py:34
  93.9 1.9 collective-permute-start.6
  95.8 17.3 %collective-permute-done.6 = bf16[16,1,32,512]{3,0,2,1:T(8,128)(2,1)S(1)} collective-permute-done((bf16[16,1,32,512]{3,0,2,1:T(8,128)(2,1)S(1)}, bf16[16,1,32,512]{3,0,2,1:T(8,128)(2,1)S(1)}, u32[]{:S(2)}, u32[]{:S(2)}) %collective-permute-start.6) | collective-permute-done | bytes 524320 | tf_op jit(solution)/shard_map/ppermute | solution.py:10
  113.2 1.7 collective-permute-start.7
  115.0 2.3 collective-permute-done.7
  117.2 8.6 %maximum_convert_fusion.3 = bf16[16,2,16,1024]{3,0,2,1:T(8,128)(2,1)S(1)} fusion(bf16[3,3,512,1024]{3,2,1,0:T(8,128)(2,1)} %param.22, bf16[16,4,32,512]{3,0,2,1:T(8,128)(2,1)S(1)} %maximum_convert_fusion, bf16[16,1,32,512]{3,0,2,1:T(8,128)(2,1)S(1)} %collective-permute-done.6, bf16[16,5,1,512]{3,0,2,1:T(8,128)(2,1)S(1)} %collective-permute-done.7, ...), kind=kOutput, calls=%fused_computation.43 | convolution fusion | flops 4836114432 | bytes 13193216 | tf_op jit(solution)/shard_map/conv_general_dilated | solution.py:34
  126.0 2.1 collective-permute-start.8
  128.0 7.6 %collective-permute-start.9 = (bf16[16,1,16,1024]{3,0,2,1:T(8,128)(2,1)S(1)}, bf16[16,1,16,1024]{3,0,2,1:T(8,128)(2,1)S(1)}, u32[]{:S(2)}, u32[]{:S(2)}) collective-permute-start(bf16[16,1,16,1024]{3,0,2,1:T(8,128)(2,1)S(1)} %get-tuple-element.14), channel_id=1, source_target_pairs={{1,0},{2,1},{3,2},{4,3},{5,4},{6,5},{7,6},{8,7},{9,8},{10,9},{11,1... | collective-permute-start | bytes 1572872 | tf_op jit(solution)/shard_map/ppermute | solution.py:14
  135.6 9.9 %collective-permute-done.8 = bf16[16,1,16,1024]{3,0,2,1:T(8,128)(2,1)S(1)} collective-permute-done((bf16[16,1,16,1024]{3,0,2,1:T(8,128)(2,1)S(1)}, bf16[16,1,16,1024]{3,0,2,1:T(8,128)(2,1)S(1)}, u32[]{:S(2)}, u32[]{:S(2)}) %collective-permute-start.8) | collective-permute-done | bytes 524320 | tf_op jit(solution)/shard_map/ppermute | solution.py:10
  147.8 3.7 %collective-permute-start.11 = (bf16[16,4,1,1024]{3,0,2,1:T(8,128)(2,1)S(1)}, bf16[16,4,1,1024]{3,0,2,1:T(8,128)(2,1)S(1)}, u32[]{:S(2)}, u32[]{:S(2)}) collective-permute-start(bf16[16,4,1,1024]{3,0,2,1:T(8,128)(2,1)S(1)} %get-tuple-element.8), channel_id=1, source_target_pairs={{64,0},{65,1},{66,2},{67,3},{68,4},{69,5},{70,6},{71,7},{72,8},{73... | collective-permute-start | bytes 393224 | tf_op jit(solution)/shard_map/ppermute | solution.py:14
  152.4 9.9 %maximum_convert_fusion.2 = bf16[16,2,16,1024]{3,0,2,1:T(8,128)(2,1)S(1)} fusion(f32[16,2,16,1024]{3,0,2,1:T(8,128)S(1)} %fusion.62, bf16[3,3,1024,1024]{3,2,1,0:T(8,128)(2,1)S(1)} %bitcast.27, bf16[16,4,1,1024]{3,0,2,1:T(8,128)(2,1)S(1)} %collective-permute-done.11, bf16[16,1,16,1024]{3,0,2,1:T(8,128)(2,1)S(1)} %collective-permute-done.9, ...), kind=kOutput, calls=%fused_computation.42 | convolution fusion | flops 9670492160 | bytes 24383488 | tf_op jit(solution)/shard_map/conv_general_dilated | solution.py:34
  162.4 1.9 collective-permute-start.12
  164.3 18.3 %collective-permute-done.12 = bf16[16,1,16,1024]{3,0,2,1:T(8,128)(2,1)S(1)} collective-permute-done((bf16[16,1,16,1024]{3,0,2,1:T(8,128)(2,1)S(1)}, bf16[16,1,16,1024]{3,0,2,1:T(8,128)(2,1)S(1)}, u32[]{:S(2)}, u32[]{:S(2)}) %collective-permute-start.12) | collective-permute-done | bytes 524320 | tf_op jit(solution)/shard_map/ppermute | solution.py:10
  182.7 1.6 collective-permute-start.13
  184.3 2.2 collective-permute-done.13
  186.5 14.0 %fusion.30 = bf16[16,1,8,2048]{3,0,2,1:T(8,128)(2,1)S(1)} fusion(bf16[3,3,1024,2048]{3,2,1,0:T(8,128)(2,1)} %param.27, bf16[16,2,16,1024]{3,0,2,1:T(8,128)(2,1)S(1)} %maximum_convert_fusion.2, bf16[16,1,16,1024]{3,0,2,1:T(8,128)(2,1)S(1)} %collective-permute-done.12, bf16[16,3,1,1024]{3,0,2,1:T(8,128)(2,1)S(1)} %collective-permute-done.13, ...), kind=kOutput, calls=%fused_computation.30 | convolution fusion | flops 4834295808 | bytes 39952384 | tf_op jit(solution)/shard_map/conv_general_dilated | solution.py:34
  200.5 1.9 collective-permute-start.14
  202.4 7.8 %collective-permute-start.15 = (bf16[16,1,8,2048]{3,0,2,1:T(8,128)(2,1)S(1)}, bf16[16,1,8,2048]{3,0,2,1:T(8,128)(2,1)S(1)}, u32[]{:S(2)}, u32[]{:S(2)}) collective-permute-start(bf16[16,1,8,2048]{3,0,2,1:T(8,128)(2,1)S(1)} %fusion.30), channel_id=1, source_target_pairs={{1,0},{2,1},{3,2},{4,3},{5,4},{6,5},{7,6},{8,7},{9,8},{10,9},{11,1... | collective-permute-start | bytes 1572872 | tf_op jit(solution)/shard_map/ppermute | solution.py:14
  210.2 9.7 %collective-permute-done.14 = bf16[16,1,8,2048]{3,0,2,1:T(8,128)(2,1)S(1)} collective-permute-done((bf16[16,1,8,2048]{3,0,2,1:T(8,128)(2,1)S(1)}, bf16[16,1,8,2048]{3,0,2,1:T(8,128)(2,1)S(1)}, u32[]{:S(2)}, u32[]{:S(2)}) %collective-permute-start.14) | collective-permute-done | bytes 524320 | tf_op jit(solution)/shard_map/ppermute | solution.py:10
  222.1 3.7 %collective-permute-start.17 = (bf16[16,3,1,2048]{3,0,2,1:T(8,128)(2,1)S(1)}, bf16[16,3,1,2048]{3,0,2,1:T(8,128)(2,1)S(1)}, u32[]{:S(2)}, u32[]{:S(2)}) collective-permute-start(bf16[16,3,1,2048]{3,0,2,1:T(8,128)(2,1)S(1)} %get-tuple-element.12), channel_id=1, source_target_pairs={{64,0},{65,1},{66,2},{67,3},{68,4},{69,5},{70,6},{71,7},{72,8},{73... | collective-permute-start | bytes 589832 | tf_op jit(solution)/shard_map/ppermute | solution.py:14
  226.9 25.7 %fusion.31 = bf16[16,1,8,2048]{3,0,2,1:T(8,128)(2,1)S(1)} fusion(f32[16,1,8,2048]{3,0,2,1:T(8,128)S(1)} %fusion.24, bf16[3,3,2048,2048]{3,2,1,0:T(8,128)(2,1)} %param.29, bf16[16,3,1,2048]{3,0,2,1:T(8,128)(2,1)S(1)} %collective-permute-done.17, bf16[16,1,8,2048]{3,0,2,1:T(8,128)(2,1)S(1)} %collective-permute-done.15, ...), kind=kOutput, calls=%fused_computation.31 | convolution fusion | flops 9668657152 | bytes 79044608 | tf_op jit(solution)/shard_map/conv_general_dilated | solution.py:34
  (68 shorter events, 13.3 us)
Async XLA Ops:
  0.0 29.3 %copy-start = (bf16[3,3,256,512]{3,2,1,0:T(8,128)(2,1)S(1)}, bf16[3,3,256,512]{3,2,1,0:T(8,128)(2,1)}, u32[]{:S(2)}) copy-start(bf16[3,3,256,512]{3,2,1,0:T(8,128)(2,1)} %param.17) | copy-start | bytes 7077892
  1.5 18.9 %collective-permute-start = (bf16[16,1,64,256]{3,0,2,1:T(8,128)(2,1)S(1)}, bf16[16,1,64,256]{3,0,2,1:T(8,128)(2,1)S(1)}, u32[]{:S(2)}, u32[]{:S(2)}) collective-permute-start(bf16[16,1,64,256]{3,0,2,1:T(8,128)(2,1)S(1)} %copy.36), channel_id=1, source_target_pairs={{0,1},{1,2},{2,3},{3,4},{4,5},{5,6},{6,7},{7,8},{8,9},{9,10},{10,1... | collective-permute-start | bytes 1572872 | tf_op jit(solution)/shard_map/ppermute | solution.py:10
  25.3 4.1 %collective-permute-start.1 = (bf16[16,9,1,256]{3,0,2,1:T(8,128)(2,1)S(1)}, bf16[16,9,1,256]{3,0,2,1:T(8,128)(2,1)S(1)}, u32[]{:S(2)}, u32[]{:S(2)}) collective-permute-start(bf16[16,9,1,256]{3,0,2,1:T(8,128)(2,1)S(1)} %slice.78), channel_id=1, source_target_pairs={{0,64},{1,65},{2,66},{3,67},{4,68},{5,69},{6,70},{7,71},{8,72},{9,... | collective-permute-start | bytes 221192 | tf_op jit(solution)/shard_map/ppermute | solution.py:10
  35.9 43.9 %copy-start.7 = (bf16[256,512]{1,0:T(8,128)(2,1)S(1)}, bf16[256,512]{1,0:T(8,128)(2,1)}, u32[]{:S(2)}) copy-start(bf16[256,512]{1,0:T(8,128)(2,1)} %param.21) | copy-start | bytes 786436
  36.9 37.5 %copy-start.4 = (bf16[16,4,32,512]{3,0,2,1:T(8,128)(2,1)S(1)}, bf16[16,4,32,512]{3,0,2,1:T(8,128)(2,1)}, u32[]{:S(2)}) copy-start(bf16[16,4,32,512]{3,0,2,1:T(8,128)(2,1)} %copy-done.3) | copy-start | bytes 6291460
  36.9 37.5 %collective-permute-start.2 = (bf16[16,1,32,512]{3,0,2,1:T(8,128)(2,1)}, bf16[16,1,32,512]{3,0,2,1:T(8,128)(2,1)}, u32[]{:S(2)}, u32[]{:S(2)}) collective-permute-start(bf16[16,1,32,512]{3,0,2,1:T(8,128)(2,1)} %get-tuple-element.9), channel_id=1, source_target_pairs={{0,1},{1,2},{2,3},{3,4},{4,5},{5,6},{6,7},{7,8},{8,9},{9,10},{10,1... | collective-permute-start | bytes 1572872 | tf_op jit(solution)/shard_map/ppermute | solution.py:10
  39.0 35.5 %collective-permute-start.3 = (bf16[16,1,32,512]{3,0,2,1:T(8,128)(2,1)}, bf16[16,1,32,512]{3,0,2,1:T(8,128)(2,1)}, u32[]{:S(2)}, u32[]{:S(2)}) collective-permute-start(bf16[16,1,32,512]{3,0,2,1:T(8,128)(2,1)} %get-tuple-element.10), channel_id=1, source_target_pairs={{1,0},{2,1},{3,2},{4,3},{5,4},{6,5},{7,6},{8,7},{9,8},{10,9},{11,1... | collective-permute-start | bytes 1572872 | tf_op jit(solution)/shard_map/ppermute | solution.py:14
  75.3 5.3 %collective-permute-start.4 = (bf16[16,6,1,512]{3,0,2,1:T(8,128)(2,1)S(1)}, bf16[16,6,1,512]{3,0,2,1:T(8,128)(2,1)S(1)}, u32[]{:S(2)}, u32[]{:S(2)}) collective-permute-start(bf16[16,6,1,512]{3,0,2,1:T(8,128)(2,1)S(1)} %get-tuple-element.5), channel_id=1, source_target_pairs={{0,64},{1,65},{2,66},{3,67},{4,68},{5,69},{6,70},{7,71},{8,72},{9,... | collective-permute-start | bytes 294920 | tf_op jit(solution)/shard_map/ppermute | solution.py:10
  76.7 4.0 %collective-permute-start.5 = (bf16[16,6,1,512]{3,0,2,1:T(8,128)(2,1)S(1)}, bf16[16,6,1,512]{3,0,2,1:T(8,128)(2,1)S(1)}, u32[]{:S(2)}, u32[]{:S(2)}) collective-permute-start(bf16[16,6,1,512]{3,0,2,1:T(8,128)(2,1)S(1)} %get-tuple-element.6), channel_id=1, source_target_pairs={{64,0},{65,1},{66,2},{67,3},{68,4},{69,5},{70,6},{71,7},{72,8},{73... | collective-permute-start | bytes 294920 | tf_op jit(solution)/shard_map/ppermute | solution.py:14
  93.9 23.4 %copy-start.10 = (f32[1024]{0:T(1024)S(1)}, f32[1024]{0:T(1024)}, u32[]{:S(2)}) copy-start(f32[1024]{0:T(1024)} %param.23) | copy-start | bytes 12292
  93.9 19.2 %collective-permute-start.6 = (bf16[16,1,32,512]{3,0,2,1:T(8,128)(2,1)S(1)}, bf16[16,1,32,512]{3,0,2,1:T(8,128)(2,1)S(1)}, u32[]{:S(2)}, u32[]{:S(2)}) collective-permute-start(bf16[16,1,32,512]{3,0,2,1:T(8,128)(2,1)S(1)} %slice.81), channel_id=1, source_target_pairs={{0,1},{1,2},{2,3},{3,4},{4,5},{5,6},{6,7},{7,8},{8,9},{9,10},{10,1... | collective-permute-start | bytes 1572872 | tf_op jit(solution)/shard_map/ppermute | solution.py:10
  113.1 39.3 %slice-start = ((s8[18874368]{0:T(1024)(128)(4,1)}), s8[4194304]{0:T(1024)(128)(4,1)S(1)}, s32[]{:S(2)}) async-start(s8[18874368]{0:T(1024)(128)(4,1)} %bitcast.26), calls=%async_computation | async-start | bytes 8388608
  113.2 39.2 %slice-start.1 = ((s8[18874368]{0:T(1024)(128)(4,1)}), s8[4194304]{0:T(1024)(128)(4,1)S(1)}, s32[]{:S(2)}) async-start(s8[18874368]{0:T(1024)(128)(4,1)} %bitcast.26), calls=%async_computation.1 | async-start | bytes 8388608
  113.2 39.2 %slice-start.2 = ((s8[18874368]{0:T(1024)(128)(4,1)}), s8[4194304]{0:T(1024)(128)(4,1)S(1)}, s32[]{:S(2)}) async-start(s8[18874368]{0:T(1024)(128)(4,1)} %bitcast.26), calls=%async_computation.2 | async-start | bytes 8388608
  113.2 39.2 %slice-start.3 = ((s8[18874368]{0:T(1024)(128)(4,1)}), s8[4194304]{0:T(1024)(128)(4,1)S(1)}, s32[]{:S(2)}) async-start(s8[18874368]{0:T(1024)(128)(4,1)} %bitcast.26), calls=%async_computation.3 | async-start | bytes 8388608
  113.2 39.2 %slice-start.4 = ((s8[18874368]{0:T(1024)(128)(4,1)}), s8[2097152]{0:T(1024)(128)(4,1)S(1)}, s32[]{:S(2)}) async-start(s8[18874368]{0:T(1024)(128)(4,1)} %bitcast.26), calls=%async_computation.4 | async-start | bytes 4194304
  113.2 4.0 %collective-permute-start.7 = (bf16[16,5,1,512]{3,0,2,1:T(8,128)(2,1)S(1)}, bf16[16,5,1,512]{3,0,2,1:T(8,128)(2,1)S(1)}, u32[]{:S(2)}, u32[]{:S(2)}) collective-permute-start(bf16[16,5,1,512]{3,0,2,1:T(8,128)(2,1)S(1)} %pad_maximum_fusion.10), channel_id=1, source_target_pairs={{0,64},{1,65},{2,66},{3,67},{4,68},{5,69},{6,70},{7,71},{8,72},{9,... | collective-permute-start | bytes 245768 | tf_op jit(solution)/shard_map/ppermute | solution.py:10
  125.8 25.6 %copy-start.6 = (bf16[512,1024]{1,0:T(8,128)(2,1)S(1)}, bf16[512,1024]{1,0:T(8,128)(2,1)}, u32[]{:S(2)}) copy-start(bf16[512,1024]{1,0:T(8,128)(2,1)} %param.26) | copy-start | bytes 3145732
  125.9 26.5 %copy-start.11 = (f32[1024]{0:T(1024)S(1)}, f32[1024]{0:T(1024)}, u32[]{:S(2)}) copy-start(f32[1024]{0:T(1024)} %param.25) | copy-start | bytes 12292
  126.0 19.6 %collective-permute-start.8 = (bf16[16,1,16,1024]{3,0,2,1:T(8,128)(2,1)S(1)}, bf16[16,1,16,1024]{3,0,2,1:T(8,128)(2,1)S(1)}, u32[]{:S(2)}, u32[]{:S(2)}) collective-permute-start(bf16[16,1,16,1024]{3,0,2,1:T(8,128)(2,1)S(1)} %get-tuple-element.13), channel_id=1, source_target_pairs={{0,1},{1,2},{2,3},{3,4},{4,5},{5,6},{6,7},{7,8},{8,9},{9,10},{10,1... | collective-permute-start | bytes 1572872 | tf_op jit(solution)/shard_map/ppermute | solution.py:10
  128.0 18.4 %collective-permute-start.9 = (bf16[16,1,16,1024]{3,0,2,1:T(8,128)(2,1)S(1)}, bf16[16,1,16,1024]{3,0,2,1:T(8,128)(2,1)S(1)}, u32[]{:S(2)}, u32[]{:S(2)}) collective-permute-start(bf16[16,1,16,1024]{3,0,2,1:T(8,128)(2,1)S(1)} %get-tuple-element.14), channel_id=1, source_target_pairs={{1,0},{2,1},{3,2},{4,3},{5,4},{6,5},{7,6},{8,7},{9,8},{10,9},{11,1... | collective-permute-start | bytes 1572872 | tf_op jit(solution)/shard_map/ppermute | solution.py:14
  146.5 5.7 %collective-permute-start.10 = (bf16[16,4,1,1024]{3,0,2,1:T(8,128)(2,1)S(1)}, bf16[16,4,1,1024]{3,0,2,1:T(8,128)(2,1)S(1)}, u32[]{:S(2)}, u32[]{:S(2)}) collective-permute-start(bf16[16,4,1,1024]{3,0,2,1:T(8,128)(2,1)S(1)} %get-tuple-element.7), channel_id=1, source_target_pairs={{0,64},{1,65},{2,66},{3,67},{4,68},{5,69},{6,70},{7,71},{8,72},{9,... | collective-permute-start | bytes 393224 | tf_op jit(solution)/shard_map/ppermute | solution.py:10
  147.8 4.6 %collective-permute-start.11 = (bf16[16,4,1,1024]{3,0,2,1:T(8,128)(2,1)S(1)}, bf16[16,4,1,1024]{3,0,2,1:T(8,128)(2,1)S(1)}, u32[]{:S(2)}, u32[]{:S(2)}) collective-permute-start(bf16[16,4,1,1024]{3,0,2,1:T(8,128)(2,1)S(1)} %get-tuple-element.8), channel_id=1, source_target_pairs={{64,0},{65,1},{66,2},{67,3},{68,4},{69,5},{70,6},{71,7},{72,8},{73... | collective-permute-start | bytes 393224 | tf_op jit(solution)/shard_map/ppermute | solution.py:14
  152.2 34.3 %copy-start.8 = (f32[2048]{0:T(1024)S(1)}, f32[2048]{0:T(1024)}, u32[]{:S(2)}) copy-start(f32[2048]{0:T(1024)} %param.28) | copy-start | bytes 24580
  162.4 20.3 %collective-permute-start.12 = (bf16[16,1,16,1024]{3,0,2,1:T(8,128)(2,1)S(1)}, bf16[16,1,16,1024]{3,0,2,1:T(8,128)(2,1)S(1)}, u32[]{:S(2)}, u32[]{:S(2)}) collective-permute-start(bf16[16,1,16,1024]{3,0,2,1:T(8,128)(2,1)S(1)} %slice.84), channel_id=1, source_target_pairs={{0,1},{1,2},{2,3},{3,4},{4,5},{5,6},{6,7},{7,8},{8,9},{9,10},{10,1... | collective-permute-start | bytes 1572872 | tf_op jit(solution)/shard_map/ppermute | solution.py:10
  182.7 43.2 %copy-start.2 = (bf16[1024,2048]{1,0:T(8,128)(2,1)S(1)}, bf16[1024,2048]{1,0:T(8,128)(2,1)}, u32[]{:S(2)}) copy-start(bf16[1024,2048]{1,0:T(8,128)(2,1)} %param.31) | copy-start | bytes 12582916
  182.7 3.8 %collective-permute-start.13 = (bf16[16,3,1,1024]{3,0,2,1:T(8,128)(2,1)S(1)}, bf16[16,3,1,1024]{3,0,2,1:T(8,128)(2,1)S(1)}, u32[]{:S(2)}, u32[]{:S(2)}) collective-permute-start(bf16[16,3,1,1024]{3,0,2,1:T(8,128)(2,1)S(1)} %pad_maximum_fusion.6), channel_id=1, source_target_pairs={{0,64},{1,65},{2,66},{3,67},{4,68},{5,69},{6,70},{7,71},{8,72},{9,... | collective-permute-start | bytes 294920 | tf_op jit(solution)/shard_map/ppermute | solution.py:10
  200.5 19.4 %collective-permute-start.14 = (bf16[16,1,8,2048]{3,0,2,1:T(8,128)(2,1)S(1)}, bf16[16,1,8,2048]{3,0,2,1:T(8,128)(2,1)S(1)}, u32[]{:S(2)}, u32[]{:S(2)}) collective-permute-start(bf16[16,1,8,2048]{3,0,2,1:T(8,128)(2,1)S(1)} %fusion.30), channel_id=1, source_target_pairs={{0,1},{1,2},{2,3},{3,4},{4,5},{5,6},{6,7},{7,8},{8,9},{9,10},{10,1... | collective-permute-start | bytes 1572872 | tf_op jit(solution)/shard_map/ppermute | solution.py:10
  202.4 18.4 %collective-permute-start.15 = (bf16[16,1,8,2048]{3,0,2,1:T(8,128)(2,1)S(1)}, bf16[16,1,8,2048]{3,0,2,1:T(8,128)(2,1)S(1)}, u32[]{:S(2)}, u32[]{:S(2)}) collective-permute-start(bf16[16,1,8,2048]{3,0,2,1:T(8,128)(2,1)S(1)} %fusion.30), channel_id=1, source_target_pairs={{1,0},{2,1},{3,2},{4,3},{5,4},{6,5},{7,6},{8,7},{9,8},{10,9},{11,1... | collective-permute-start | bytes 1572872 | tf_op jit(solution)/shard_map/ppermute | solution.py:14
  220.8 5.8 %collective-permute-start.16 = (bf16[16,3,1,2048]{3,0,2,1:T(8,128)(2,1)S(1)}, bf16[16,3,1,2048]{3,0,2,1:T(8,128)(2,1)S(1)}, u32[]{:S(2)}, u32[]{:S(2)}) collective-permute-start(bf16[16,3,1,2048]{3,0,2,1:T(8,128)(2,1)S(1)} %get-tuple-element.11), channel_id=1, source_target_pairs={{0,64},{1,65},{2,66},{3,67},{4,68},{5,69},{6,70},{7,71},{8,72},{9,... | collective-permute-start | bytes 589832 | tf_op jit(solution)/shard_map/ppermute | solution.py:10
  222.1 4.7 %collective-permute-start.17 = (bf16[16,3,1,2048]{3,0,2,1:T(8,128)(2,1)S(1)}, bf16[16,3,1,2048]{3,0,2,1:T(8,128)(2,1)S(1)}, u32[]{:S(2)}, u32[]{:S(2)}) collective-permute-start(bf16[16,3,1,2048]{3,0,2,1:T(8,128)(2,1)S(1)} %get-tuple-element.12), channel_id=1, source_target_pairs={{64,0},{65,1},{66,2},{67,3},{68,4},{69,5},{70,6},{71,7},{72,8},{73... | collective-permute-start | bytes 589832 | tf_op jit(solution)/shard_map/ppermute | solution.py:14
  226.9 26.8 %copy-start.1 = (bf16[3,3,256,512]{3,2,1,0:T(8,128)(2,1)S(1)}, bf16[3,3,256,512]{3,2,1,0:T(8,128)(2,1)}, u32[]{:S(2)}) copy-start(bf16[3,3,256,512]{3,2,1,0:T(8,128)(2,1)} %param.17) | copy-start | bytes 7077892
  (5 other events, 27.1 us)
where the time goes:
time: 258 us; the launch traced here: 254 us
  waiting for transfers between devices  80.6 us (31%)
  matrix products  78.8 us (31%)
  starting transfers between devices  54.9 us (21%)
  local copies, waits for them, and re-layouts  37.9 us (15%)
    ppermute x12, waiting for transfers between devices, from_lower(): lax.ppermute(edge_part, axis_name, [(dev_index, dev_index + 1) for dev_in...  78.3 us
    conv_general_dilated x6, matrix products, conv_valid(): lax.conv_general_dilated(act_in, weight, (stride, stride), 'VALID', dimen...  76.5 us
    ppermute x6, starting transfers between devices, from_upper(): lax.ppermute(edge_part, axis_name, [(dev_index + 1, dev_index) for dev_in...  33.4 us
    slice x1, local copies, waits for them, and re-layouts, basic_block(): z_prev[:, ::2, ::2]  27.8 us
    ppermute x12, starting transfers between devices, from_lower(): lax.ppermute(edge_part, axis_name, [(dev_index, dev_index + 1) for dev_in...  21.6 us
  transfers between devices with their start and end apart: 18, of which 12 were waited for; matrix products, arithmetic and copies ran while one was open for 12% of the time, Pallas kernels for 0%

commit v1 on v0

v1 whole, which is shorter than its diff:
```python
import jax
import jax.numpy as jnp
from jax import lax
from jax.experimental import pallas as pl
from jax.experimental.pallas import tpu as pltpu
from jax.sharding import PartitionSpec as P

F32 = jnp.float32
BF16 = jnp.bfloat16
RING = 8
GROUPS = (
    [("down", 2, kx, 0) for kx in range(3)]
    + [("down", 1, kx, 0) for kx in range(3)]
    + [("proj", 0, 0, 0)]
    + [("down", 0, kx, 0) for kx in range(3)]
    + [("conv", ky, kx, kh) for ky in (1, 0, 2) for kx in range(3) for kh in range(2)]
)
CONV_0 = 10


def encoder_kernel(rows, cols, x_ref, wd1, wc1, wp1, wd2, wc2, wp2, wd3, wc3, wp3, bd1, bc1, bd2, bc2, bd3, bc3, out_ref,
                   xp, y1p, z1p, y2p, z2p, y3p, vd1, vc1, vp1, ring, acc, out_v, load_sem, w2_sem, ring_sem, send_sem, recv_sem):
    r = lax.axis_index("row")
    c = lax.axis_index("col")
    has_up = r > 0
    has_down = r < rows - 1
    images = x_ref.shape[3]
    part = acc.shape[2]

    c1, c2, c3 = wd1.shape[2], wd2.shape[2], wd3.shape[2]

    def ring_view(chunk, base):
        slot, sub = base + chunk // 4, chunk % 4
        return ring.at[slot, pl.ds((sub // 2) * c1, c1), pl.ds((sub % 2) * c2, c2)]

    def ring_block(chunk, base, n0):
        slot, sub = base + chunk // 4, chunk % 4
        return ring[slot, pl.ds((sub // 2) * c1, c1), pl.ds((sub % 2) * c2 + n0, part)]

    load_x = pltpu.make_async_copy(x_ref, xp.at[pl.ds(1, 8), pl.ds(1, x_ref.shape[1])], load_sem.at[0])
    load_d1 = pltpu.make_async_copy(wd1, vd1, load_sem.at[1])
    load_c1 = pltpu.make_async_copy(wc1, vc1, load_sem.at[2])
    load_p1 = pltpu.make_async_copy(wp1, vp1, load_sem.at[3])
    loads_d2 = [pltpu.make_async_copy(wd2.at[t], ring_view(t, 0), w2_sem.at[t]) for t in range(9)]
    loads_d2.append(pltpu.make_async_copy(wp2, ring_view(9, 0), w2_sem.at[9]))
    loads_c2 = [pltpu.make_async_copy(wc2.at[q // 2, pl.ds((q % 2) * c1, c1)], ring_view(q, 3), w2_sem.at[10 + q]) for q in range(18)]

    def group_copy(g):
        kind, ky, kx, kh = GROUPS[g]
        if kind == "down":
            src = wd3.at[ky * 3 + kx]
        elif kind == "proj":
            src = wp3
        else:
            src = wc3.at[ky * 3 + kx, pl.ds(kh * c2, c2)]
        return pltpu.make_async_copy(src, ring.at[g % RING], ring_sem.at[g % RING])

    up, down = jnp.maximum(r - 1, 0), jnp.minimum(r + 1, rows - 1)
    copies = []

    def halo(src, dst, row, col, send_if, recv_if):
        index = len(copies)
        copy = pltpu.make_async_remote_copy(src_ref=src, dst_ref=dst, send_sem=send_sem.at[index], recv_sem=recv_sem.at[index],
                                            device_id={"row": row, "col": col}, device_id_type=pl.DeviceIdType.MESH)
        copies.append((copy, send_if))

        def start():
            if send_if is None:
                copy.start()
            else:
                pl.when(send_if)(copy.start)

        def arrive():
            if recv_if is None:
                copy.wait_recv()
            else:
                pl.when(recv_if)(copy.wait_recv)

        return start, arrive

    is_left = c == 0
    is_right = c == 1
    other = 1 - c

    def pair_row(src_row, buf):
        w = buf.shape[1] - 1
        return halo(src_row, buf.at[0, pl.ds(1, w)], down, c, has_down, has_up)

    def pair_diag(src_pixel, buf):
        return halo(src_pixel, buf.at[0, 0, 1], down, other, has_down & is_left, has_up & is_right)

    def pair_col(src_col, dst_col):
        return halo(src_col, dst_col, r, other, is_left, is_right)

    def plain_row(buf, towards_down):
        n, w = buf.shape[0], buf.shape[1]
        if towards_down:
            return halo(buf.at[n - 2, pl.ds(1, w - 2)], buf.at[0, pl.ds(1, w - 2)], down, c, has_down, has_up)
        return halo(buf.at[1, pl.ds(1, w - 2)], buf.at[n - 1, pl.ds(1, w - 2)], up, c, has_up, has_down)

    def plain_edge(buf):
        w = buf.shape[1]
        return (w - 2) - (w - 3) * c, (w - 1) * c

    def plain_diag(buf, towards_down):
        n = buf.shape[0]
        src_col, dst_col = plain_edge(buf)
        if towards_down:
            return halo(buf.at[n - 2, src_col], buf.at[0, dst_col], down, other, has_down, has_up)
        return halo(buf.at[1, src_col], buf.at[n - 1, dst_col], up, other, has_up, has_down)

    def plain_col(buf, first, count):
        src_col, dst_col = plain_edge(buf)
        return halo(buf.at[pl.ds(first, count), src_col], buf.at[pl.ds(first, count), dst_col], r, other, None, None)

    w1, w2, w3 = y1p.shape[1] - 2, y2p.shape[1] - 2, y3p.shape[1] - 2
    x_row = pair_row(x_ref.at[7], xp)
    x_diag = pair_diag(x_ref.at[7, w1 - 1, 1], xp)
    x_col = pair_col(x_ref.at[pl.ds(0, 8), w1 - 1, 1], xp.at[pl.ds(1, 8), 0, 1])
    y1_down, y1_up = plain_row(y1p, True), plain_row(y1p, False)
    y1_ddown, y1_dup = plain_diag(y1p, True), plain_diag(y1p, False)
    y1_col_b, y1_col_a = plain_col(y1p, 2, 3), plain_col(y1p, 1, 1)
    z1_row = pair_row(z1p.at[4, pl.ds(1, w1 // 2)], z1p)
    z1_diag = pair_diag(z1p.at[4, w1 // 2, 1], z1p)
    z1_cols = [pair_col(z1p.at[pl.ds(a, n), w1 // 2, 1], z1p.at[pl.ds(a, n), 0, 1]) for a, n in ((1, 1), (2, 2), (4, 1))]
    y2_down, y2_up = plain_row(y2p, True), plain_row(y2p, False)
    y2_ddown, y2_dup = plain_diag(y2p, True), plain_diag(y2p, False)
    y2_col_b, y2_col_a = plain_col(y2p, 2, 1), plain_col(y2p, 1, 1)
    z2_row = pair_row(z2p.at[2, pl.ds(1, w2 // 2)], z2p)
    z2_diag = pair_diag(z2p.at[2, w2 // 2, 1], z2p)
    z2_cols = [pair_col(z2p.at[pl.ds(a, 1), w2 // 2, 1], z2p.at[pl.ds(a, 1), 0, 1]) for a in (1, 2)]
    y3_down, y3_up = plain_row(y3p, True), plain_row(y3p, False)
    y3_ddown, y3_dup = plain_diag(y3p, True), plain_diag(y3p, False)
    y3_col = plain_col(y3p, 1, 1)

    def start(*ops):
        for op in ops:
            op[0]()

    def arrive(*ops):
        for op in ops:
            op[1]()

    for buf in (xp, z1p, z2p):
        @pl.when(has_up == False)
        def _(buf=buf):
            buf[0] = jnp.zeros(buf.shape[1:], BF16)

        @pl.when(is_left)
        def _(buf=buf):
            buf[:, 0, 1] = jnp.zeros((buf.shape[0],) + buf.shape[3:], BF16)

    for buf in (y1p, y2p, y3p):
        n, w = buf.shape[0], buf.shape[1]

        @pl.when(has_up == False)
        def _(buf=buf):
            buf[0] = jnp.zeros(buf.shape[1:], BF16)

        @pl.when(has_down == False)
        def _(buf=buf, n=n):
            buf[n - 1] = jnp.zeros(buf.shape[1:], BF16)

        @pl.when(is_left)
        def _(buf=buf):
            buf[:, 0] = jnp.zeros((buf.shape[0],) + buf.shape[2:], BF16)

        @pl.when(is_right)
        def _(buf=buf, w=w):
            buf[:, w - 1] = jnp.zeros((buf.shape[0],) + buf.shape[2:], BF16)

    load_x.start()
    load_d1.start()
    barrier = pltpu.get_barrier_semaphore()

    def signal(row, col):
        pl.semaphore_signal(barrier, inc=1, device_id={"row": row, "col": col}, device_id_type=pl.DeviceIdType.MESH)

    signal(r, other)

    @pl.when(has_up)
    def _():
        signal(up, c)
        signal(up, other)

    @pl.when(has_down)
    def _():
        signal(down, c)
        signal(down, other)

    inner = has_up & has_down

    @pl.when(inner)
    def _():
        pl.semaphore_wait(barrier, 5)

    @pl.when(inner == False)
    def _():
        pl.semaphore_wait(barrier, 3)

    start(x_col, x_diag, x_row)

    def piece(taps, n_all, slot=None, fresh=True, bias=None, store=None):
        for n0 in range(0, n_all, part):
            total = None
            for lhs, weight in taps:
                left = lhs()
                prod = jnp.dot(left, weight(n0), preferred_element_type=F32)
                total = prod if total is None else total + prod
            m = total.shape[0]
            at = pl.ds((n0 // part) * m, m)
            if not fresh:
                total = total + acc[slot, at]
            if store is None:
                acc[slot, at] = total
            else:
                store(n0, jnp.maximum(total + bias[:, pl.ds(n0, part)], 0.0).astype(BF16))

    def pair_lhs(buf, row, kx):
        w = buf.shape[1] - 1
        return lambda: buf[row, pl.ds((kx + 1) // 2, w), (kx + 1) % 2].reshape(w * images, buf.shape[4])

    def plain_lhs(buf, row, kx, k0=0, k=None):
        w = buf.shape[1] - 2
        k = k or buf.shape[3]
        return lambda: buf[row, pl.ds(kx, w), :, pl.ds(k0, k)].reshape(w * images, k)

    def down1(h, kys, **kw):
        def store(n0, value):
            y1p[h + 1, pl.ds(1, w1), :, pl.ds(n0, part)] = value.reshape(w1, images, part)
        taps = [(pair_lhs(xp, 2 * h + ky, kx), lambda n0, t=3 * ky + kx: vd1[t, :, pl.ds(n0, part)]) for ky in kys for kx in range(3)]
        piece(taps, c1, bias=bd1, store=store if kw.pop("final", True) else None, **kw)

    def conv1(h, kys, proj=False, **kw):
        def store(n0, value):
            z1p[h + 1, pl.ds(1, w1 // 2), :, :, pl.ds(n0, part)] = value.reshape(w1 // 2, 2, images, part)
        taps = [(plain_lhs(y1p, h + ky, kx), lambda n0, t=3 * ky + kx: vc1[t, :, pl.ds(n0, part)]) for ky in kys for kx in range(3)]
        if proj:
            taps.append((pair_lhs(xp, 2 * h + 1, 1), lambda n0: vp1[:, pl.ds(n0, part)]))
        piece(taps, c1, bias=bc1, store=store if kw.pop("final", True) else None, **kw)

    def down2(h, kys, **kw):
        def store(n0, value):
            y2p[h + 1, pl.ds(1, w2), :, pl.ds(n0, part)] = value.reshape(w2, images, part)
        taps = [(pair_lhs(z1p, 2 * h + ky, kx), lambda n0, t=3 * ky + kx: ring_block(t, 0, n0)) for ky in kys for kx in range(3)]
        piece(taps, c2, bias=bd2, store=store if kw.pop("final", True) else None, **kw)

    def conv2(h, kys, proj=False, **kw):
        def store(n0, value):
            z2p[h + 1, pl.ds(1, w2 // 2), :, :, pl.ds(n0, part)] = value.reshape(w2 // 2, 2, images, part)
        taps = [(plain_lhs(y2p, h + ky, kx, kh * c1, c1), lambda n0, q=2 * (3 * ky + kx) + kh: ring_block(q, 3, n0))
                for ky in kys for kx in range(3) for kh in range(2)]
        if proj:
            taps.append((pair_lhs(z1p, 2 * h + 1, 1), lambda n0: ring_block(9, 0, n0)))
        piece(taps, c2, bias=bc2, store=store if kw.pop("final", True) else None, **kw)

    m3 = w3 * images

    def group_dots(left, slot, into, fresh=False):
        for n0 in range(0, c3, part):
            at = pl.ds((n0 // part) * m3, m3)
            prod = jnp.dot(left, ring[slot, :, pl.ds(n0, part)], preferred_element_type=F32)
            acc[into, at] = prod if fresh else acc[into, at] + prod

    def stage3_group(g, into, fresh=False):
        kind, ky, kx, kh = GROUPS[g]
        group_copy(g).wait()
        left = pair_lhs(z2p, 1, 1)() if kind == "proj" else pair_lhs(z2p, ky, kx)()
        group_dots(left, g % RING, into, fresh)
        if g + RING < len(GROUPS):
            group_copy(g + RING).start()

    def conv3(ky, first):
        def body(i, carry):
            kx, kh = i // 2, lax.rem(i, 2)
            g = first + i
            slot = lax.rem(g, RING)
            pltpu.make_async_copy(wc3.at[0, pl.ds(0, c2)], ring.at[slot], ring_sem.at[slot]).wait()
            left = y3p[ky, pl.ds(kx, w3), :, pl.ds(pl.multiple_of(kh * c2, c2), c2)].reshape(m3, c2)
            group_dots(left, slot, 1)
            nxt = g + RING - CONV_0

            @pl.when(g + RING < len(GROUPS))
            def _():
                nky = jnp.where(nxt < 12, 0, 2)
                tap = 3 * nky + lax.rem(nxt, 6) // 2
                k0 = pl.multiple_of(lax.rem(nxt, 2) * c2, c2)
                pltpu.make_async_copy(wc3.at[tap, pl.ds(k0, c2)], ring.at[slot], ring_sem.at[slot]).start()
            return carry
        lax.fori_loop(0, 6, body, 0)

    load_x.wait()
    load_d1.wait()
    load_c1.start()
    load_p1.start()
    arrive(x_col)
    down1(3, (0, 1, 2))
    start(y1_ddown, y1_down)
    for copy in loads_d2:
        copy.start()
    down1(1, (0, 1, 2))
    down1(2, (0, 1, 2))
    start(y1_col_b)
    for copy in loads_c2:
        copy.start()
    down1(0, (1, 2), slot=0, final=False)
    load_c1.wait()
    load_p1.wait()
    arrive(y1_col_b)
    conv1(2, (0, 1, 2), proj=True)
    conv1(1, (1, 2), proj=True, slot=1, final=False)
    conv1(3, (0, 1), proj=True, slot=2, final=False)
    arrive(x_row, x_diag)
    down1(0, (0,), slot=0, fresh=False)
    start(y1_col_a, y1_dup, y1_up)
    arrive(y1_col_a)
    conv1(1, (0,), slot=1, fresh=False)
    start(z1_cols[1])
    conv1(0, (1, 2), proj=True, slot=0, final=False)
    for copy in loads_d2:
        copy.wait()
    arrive(z1_cols[1])
    down2(1, (0, 1), slot=1, final=False)
    arrive(y1_down, y1_ddown)
    conv1(0, (0,), slot=0, fresh=False)
    start(z1_cols[0])
    arrive(y1_up, y1_dup)
    conv1(3, (2,), slot=2, fresh=False)
    start(z1_cols[2], z1_diag, z1_row)

    arrive(z1_cols[2])
    down2(1, (2,), slot=1, fresh=False)
    start(y2_col_b, y2_ddown, y2_down)
    arrive(z1_cols[0])
    down2(0, (1, 2), slot=0, final=False)
    for copy in loads_c2:
        copy.wait()
    arrive(y2_col_b)
    conv2(1, (1,), proj=True, slot=1, final=False)
    conv2(0, (2,), proj=True, slot=2, final=False)
    arrive(z1_row, z1_diag)
    down2(0, (0,), slot=0, fresh=False)
    start(y2_col_a, y2_dup, y2_up)
    for g in range(3):
        group_copy(g).start()
    arrive(y2_col_a)
    conv2(1, (0,), slot=1, fresh=False, final=False)
    conv2(0, (1,), slot=2, fresh=False, final=False)
    arrive(y2_up, y2_dup)
    conv2(1, (2,), slot=1, fresh=False)
    start(z2_cols[1], z2_diag, z2_row)
    arrive(y2_down, y2_ddown)
    conv2(0, (0,), slot=2, fresh=False)
    start(z2_cols[0])
    for g in range(3, RING):
        group_copy(g).start()

    arrive(z2_cols[1])
    for g in range(3):
        stage3_group(g, 0, fresh=g == 0)
    arrive(z2_cols[0])
    for g in range(3, 6):
        stage3_group(g, 0)
    stage3_group(6, 1, fresh=True)
    arrive(z2_row, z2_diag)
    for g in range(7, 10):
        stage3_group(g, 0)
    for n0 in range(0, c3, part):
        total = acc[0, pl.ds((n0 // part) * m3, m3)] + bd3[:, pl.ds(n0, part)]
        y3p[1, pl.ds(1, w3), :, pl.ds(n0, part)] = jnp.maximum(total, 0.0).astype(BF16).reshape(w3, images, part)
    start(y3_col, y3_ddown, y3_dup, y3_down, y3_up)
    arrive(y3_col)
    conv3(1, CONV_0)
    arrive(y3_down, y3_ddown)
    conv3(0, CONV_0 + 6)
    arrive(y3_up, y3_dup)
    conv3(2, CONV_0 + 12)
    for n0 in range(0, c3, part):
        total = acc[1, pl.ds((n0 // part) * m3, m3)] + bc3[:, pl.ds(n0, part)]
        out_v[:, :, pl.ds(n0, part)] = jnp.maximum(total, 0.0).astype(BF16).reshape(w3, images, part)
    put = pltpu.make_async_copy(out_v, out_ref, load_sem.at[0])
    put.start()
    for copy, send_if in copies:
        if send_if is None:
            copy.wait_send()
        else:
            pl.when(send_if)(copy.wait_send)
    put.wait()


def solution(mesh):
    row_count = mesh.shape["row"]
    col_count = mesh.shape["col"]
    tile_spec = P("batch", "row", "col")

    def local_blocks(x_tile, *params):
        images, tile_h, tile_w, c0 = x_tile.shape
        x_in = x_tile.transpose(1, 2, 0, 3).reshape(tile_h, tile_w // 2, 2, images, c0)
        weights, biases = [], []
        for stage in range(3):
            w_down, b_down, w_conv, b_conv, w_proj = params[5 * stage:5 * stage + 5]
            weights += [w_down.reshape((9,) + w_down.shape[2:]), w_conv.reshape((9,) + w_conv.shape[2:]), w_proj]
            biases += [b_down.reshape(1, -1), b_conv.reshape(1, -1)]
        c1, c2, c3 = (weights[3 * stage].shape[2] for stage in range(3))
        w1, w2, w3 = tile_w // 2, tile_w // 4, tile_w // 8
        any_spec = pl.BlockSpec(memory_space=pl.ANY)
        vmem_spec = pl.BlockSpec(memory_space=pltpu.VMEM)
        copy_count = 29
        out = pl.pallas_call(
            lambda *refs: encoder_kernel(row_count, col_count, *refs),
            out_shape=jax.ShapeDtypeStruct((w3, images, c3), BF16),
            in_specs=[any_spec] * 10 + [vmem_spec] * 6,
            out_specs=any_spec,
            scratch_shapes=[
                pltpu.VMEM((tile_h + 1, w1 + 1, 2, images, c0), BF16),
                pltpu.VMEM((6, w1 + 2, images, c1), BF16),
                pltpu.VMEM((5, w2 + 1, 2, images, c1), BF16),
                pltpu.VMEM((4, w2 + 2, images, c2), BF16),
                pltpu.VMEM((3, w3 + 1, 2, images, c2), BF16),
                pltpu.VMEM((3, w3 + 2, images, c3), BF16),
                pltpu.VMEM((9, c0, c1), BF16),
                pltpu.VMEM((9, c1, c1), BF16),
                pltpu.VMEM((c0, c1), BF16),
                pltpu.VMEM((RING, c2, c3), BF16),
                pltpu.VMEM((3, w1 * images, c1), F32),
                pltpu.VMEM((w3, images, c3), BF16),
                pltpu.SemaphoreType.DMA((4,)),
                pltpu.SemaphoreType.DMA((28,)),
                pltpu.SemaphoreType.DMA((RING,)),
                pltpu.SemaphoreType.DMA((copy_count,)),
                pltpu.SemaphoreType.DMA((copy_count,)),
            ],
            compiler_params=pltpu.CompilerParams(collective_id=0, has_side_effects=True, vmem_limit_bytes=67043328),
            name="encoder",
        )(x_in, *weights, *biases)
        return out.transpose(1, 0, 2).reshape(images, 1, w3, c3)

    return jax.shard_map(local_blocks, mesh=mesh, in_specs=(tile_spec,) + (P(),) * 15, out_specs=tile_spec, check_vma=False)
```

time: 258 us -> 111 us (0.43)
  the two profiles are of different devices: /device:TPU:97 before, /device:TPU:32 now
where the time goes in v1:
time: 111 us; the launch traced here: 110 us
  Pallas kernels  102 us (92%)
  local copies, waits for them, and re-layouts  8.81 us (8%)
    pallas_call x1, Pallas kernels, local_blocks(): pl.pallas_call(lambda *refs: encoder_kernel(row_count, col_count, *refs),...  102 us
    transpose x1, local copies, waits for them, and re-layouts, local_blocks(): x_tile.transpose(1, 2, 0, 3).reshape(tile_h, tile_w // 2, 2, images, c0)  6.68 us

profile of v1, /device:TPU:32, one launch (start us, length us, event | category | flops | bytes accessed | tf_op | source)
XLA Modules:
  0.0 110.5 jit_solution(24066039590037861)
XLA Ops:
  0.0 6.7 %copy.17 = bf16[8,64,16,256]{3,2,1,0:T(8,128)(2,1)} copy(bf16[8,64,16,256]{3,1,0,2:T(8,128)(2,1)} %bitcast.22) | data formatting | bytes 8388608 | tf_op jit(solution)/shard_map/transpose | solution.py:398
  6.7 101.7 %encoder.1 = bf16[8,16,2048]{2,1,0:T(8,128)(2,1)} custom-call(bf16[8,32,2,16,256]{4,3,2,1,0:T(8,128)(2,1)} %bitcast.19, bf16[9,256,512]{2,1,0:T(8,128)(2,1)} %bitcast.23, bf16[9,512,512]{2,1,0:T(8,128)(2,1)} %bitcast.21, bf16[256,512]{1,0:T(8,128)(2,1)} %refs_3_.1, bf16[9,512,1024]{2,1,0:T(8,128)(2,1)} %bitcast.20, bf16[9,1024,1024]{2,1,0:T(8,128)(2,1)} %bitcast.18, ...), custom_call_target="tpu_custom_call" | custom-call | tf_op jit(solution)/shard_map/encoder/pallas_call | solution.py:409
  108.4 2.1 %copy.18 = bf16[16,1,8,2048]{3,2,1,0:T(8,128)(2,1)} copy(bf16[16,1,8,2048]{3,0,2,1:T(8,128)(2,1)} %bitcast.24) | data formatting | bytes 1048576 | tf_op jit(solution)/shard_map/reshape | solution.py:436

commit v2 on v0

v2 whole, which is shorter than its diff:
```python
import jax
import jax.numpy as jnp
import numpy as np
from jax import lax
from jax.experimental import pallas as pl
from jax.experimental.pallas import tpu as pltpu
from jax.sharding import PartitionSpec as P

F32 = jnp.float32
BF16 = jnp.bfloat16
RING = 10
RAW = 4
TAPS = (0, 1, 2)
MID = dict(final=False)
END = dict(fresh=False)
PROJ = dict(proj=True)


def encoder_kernel(rows, cols, x_ref, wd1, wc1, wp1, wd2, wc2, wp2, wd3, wc3, wp3, bd1, bc1, bd2, bc2, bd3, bc3, perm, out_ref,
                   xp, y1p, z1p, y2p, z2p, y3p, ring, acc, out_v, raw, raw_halo, out_sem, raw_sem, w1_sem, w2_sem, ring_sem, send_sem, recv_sem):
    r = lax.axis_index("row")
    c = lax.axis_index("col")
    has_up = r > 0
    has_down = r < rows - 1
    images = x_ref.shape[0]
    part = acc.shape[2]
    c0, c1, c2, c3 = x_ref.shape[3], wd1.shape[2], wd2.shape[2], wd3.shape[2]

    def place_c1(t):
        if t == 8:
            return 9, 0, 0
        return 8, (t // 4) * c1, (t % 4) * c1

    def place_d1(t):
        return 9, (t % 4) * c0, (1 + t // 4) * c1

    def place_d2(t):
        q = (t - 3 if t < 9 else 6) if t > 2 else 8 + t
        return q // 4, ((q % 4) // 2) * c1, (q % 2) * c2

    def place_c2(tap, kh):
        q = 2 * ((tap + 6) % 9) + kh
        return 3 + q // 4, ((q % 4) // 2) * c1, (q % 2) * c2

    def load(src, place, size, sem):
        slot, k0, n0 = place
        return pltpu.make_async_copy(src, ring.at[slot, pl.ds(k0, size[0]), pl.ds(n0, size[1])], sem)

    def block(place, k, n0):
        slot, k0, n1 = place
        return ring[slot, pl.ds(k0, k), pl.ds(n1 + n0, part)]

    loads_d1 = [load(wd1.at[t], place_d1(t), (c0, c1), w1_sem.at[t]) for t in range(9)]
    loads_d1.append(load(wp1, place_d1(9), (c0, c1), w1_sem.at[9]))
    loads_c1 = [load(wc1.at[t], place_c1(t), (c1, c1), w1_sem.at[10 + t]) for t in range(9)]
    loads_d2 = [load(wd2.at[t], place_d2(t), (c1, c2), w2_sem.at[t]) for t in range(9)]
    loads_d2.append(load(wp2, place_d2(9), (c1, c2), w2_sem.at[9]))
    loads_c2 = [load(wc2.at[q // 2, pl.ds((q % 2) * c1, c1)], place_c2(q // 2, q % 2), (c1, c2), w2_sem.at[10 + q]) for q in range(18)]

    def first_groups(g):
        if g == 6:
            src = wp3
        else:
            ky = 2 if g < 3 else 1 if g < 6 else 0
            kx = g % 3 if g < 6 else g - 7
            src = wd3.at[3 * ky + kx]
        return pltpu.make_async_copy(src, ring.at[(g + 8) % RING], ring_sem.at[(g + 8) % RING])

    def conv3_copy(tap, k0, slot):
        return pltpu.make_async_copy(wc3.at[tap, pl.ds(k0, c2)], ring.at[slot], ring_sem.at[slot])

    def conv3_first(j):
        if j < 6:
            tap, kh = 3 + j // 2, j % 2
        else:
            tap, kh = 6 * ((j - 6) // 3) + (j - 6) % 3, 0
        conv3_copy(tap, kh * c2, (j + 8) % RING).start()

    def group_wait(slot):
        pltpu.make_async_copy(wc3.at[0, pl.ds(0, c2)], ring.at[slot], ring_sem.at[slot]).wait()

    up, down = jnp.maximum(r - 1, 0), jnp.minimum(r + 1, rows - 1)
    copies = []

    def halo(src, dst, row, col, send_if, recv_if):
        index = len(copies)
        copy = pltpu.make_async_remote_copy(src_ref=src, dst_ref=dst, send_sem=send_sem.at[index], recv_sem=recv_sem.at[index],
                                            device_id={"row": row, "col": col}, device_id_type=pl.DeviceIdType.MESH)
        copies.append((send_if, copy.wait_send))
        return copy, send_if, recv_if

    is_left = c == 0
    is_right = c == 1
    up_left, up_right, down_left, down_right = has_up & is_left, has_up & is_right, has_down & is_left, has_down & is_right
    other = 1 - c

    w1, w2, w3 = y1p.shape[1] - 2, y2p.shape[1] - 2, y3p.shape[1] - 2

    def parts(w, a):
        return (0, a), (a, w - a)

    y1_parts = parts(w1, w2 + 3)
    z1_parts = parts(w1, w2 + 2)
    y2_parts = parts(w2, w3 + 1)
    z2_parts = parts(w2, w3)

    def pair_rows(buf, sections):
        n = buf.shape[0]
        ops = []
        for first, count in sections:
            cells = pl.ds(1 + first // 2, count // 2)
            ops.append(halo(buf.at[n - 1, cells], buf.at[0, cells], down, c, has_down, has_up))
        return ops

    def pair_diag(buf):
        n, w = buf.shape[0], buf.shape[1] - 1
        return halo(buf.at[n - 1, w, 1], buf.at[0, 0, 1], down, other, down_left, up_right)

    def pair_col(buf, first, count):
        w = buf.shape[1] - 1
        return halo(buf.at[pl.ds(first, count), w, 1], buf.at[pl.ds(first, count), 0, 1], r, other, is_left, is_right)

    def plain_down(buf, k0=0, k=None):
        n, w, k = buf.shape[0], buf.shape[1], k or buf.shape[3]
        at = (pl.ds(1, w - 2), pl.ds(0, images), pl.ds(k0, k))
        return halo(buf.at[(n - 2,) + at], buf.at[(0,) + at], down, c, has_down, has_up)

    def plain_ups(buf, sections, k0=0, k=None):
        n, k = buf.shape[0], k or buf.shape[3]
        ops = []
        for first, count in sections:
            at = (pl.ds(1 + first, count), pl.ds(0, images), pl.ds(k0, k))
            ops.append(halo(buf.at[(1,) + at], buf.at[(n - 1,) + at], up, c, has_up, has_down))
        return ops

    def plain_edge(buf):
        w = buf.shape[1]
        return (w - 2) - (w - 3) * c, (w - 1) * c

    def plain_diag(buf, towards_down, k0=0, k=None):
        n, k = buf.shape[0], k or buf.shape[3]
        src_col, dst_col = plain_edge(buf)
        at = (pl.ds(0, images), pl.ds(k0, k))
        if towards_down:
            return halo(buf.at[(n - 2, src_col) + at], buf.at[(0, dst_col) + at], down, other, has_down, has_up)
        return halo(buf.at[(1, src_col) + at], buf.at[(n - 1, dst_col) + at], up, other, has_up, has_down)

    def plain_col(buf, first, count, k0=0, k=None):
        k = k or buf.shape[3]
        src_col, dst_col = plain_edge(buf)
        at = (pl.ds(0, images), pl.ds(k0, k))
        return halo(buf.at[(pl.ds(first, count), src_col) + at], buf.at[(pl.ds(first, count), dst_col) + at], r, other, None, None)

    x_row = halo(x_ref.at[:, 7], raw_halo, down, c, has_down, has_up)
    x_diag = pair_diag(xp)
    x_col_b, x_col_a = pair_col(xp, 6, 3), pair_col(xp, 1, 5)
    y1_down, y1_ups = plain_down(y1p), plain_ups(y1p, y1_parts)
    y1_ddown, y1_dup = plain_diag(y1p, True), plain_diag(y1p, False)
    y1_col_b, y1_col_a = plain_col(y1p, 2, 3), plain_col(y1p, 1, 1)
    z1_rows, z1_diag = pair_rows(z1p, z1_parts), pair_diag(z1p)
    z1_cols = [pair_col(z1p, a, n) for a, n in ((1, 1), (2, 2), (4, 1))]
    y2_down, y2_ups = plain_down(y2p), plain_ups(y2p, y2_parts)
    y2_ddown, y2_dup = plain_diag(y2p, True), plain_diag(y2p, False)
    y2_col_b, y2_col_a = plain_col(y2p, 2, 1), plain_col(y2p, 1, 1)
    z2_rows, z2_diag = pair_rows(z2p, z2_parts), pair_diag(z2p)
    z2_cols = [pair_col(z2p, a, 1) for a in (1, 2)]
    y3_halves = []
    for k0 in (0, c2):
        y3_halves.append((plain_col(y3p, 1, 1, k0, c2), plain_diag(y3p, True, k0, c2), plain_diag(y3p, False, k0, c2),
                          plain_down(y3p, k0, c2), plain_ups(y3p, ((0, w3),), k0, c2)[0]))

    def under_conditions(items):
        groups = {}
        for condition, action in items:
            groups.setdefault(id(condition), (condition, []))[1].append(action)
        for condition, actions in groups.values():
            def run(actions=actions):
                for action in actions:
                    action()
            if condition is None:
                run()
            else:
                pl.when(condition)(run)

    def start(*ops):
        under_conditions([(send_if, copy.start) for copy, send_if, _ in ops])

    def arrive(*ops):
        under_conditions([(recv_if, copy.wait_recv) for copy, _, recv_if in ops])

    def start_with_diag(row, diag, last):
        under_conditions([(has_up, row[0].start), (up_left if last else up_right, diag[0].start)])

    def arrive_with_diag(row, diag, last):
        under_conditions([(has_down, row[0].wait_recv), (down_left if last else down_right, diag[0].wait_recv)])

    pair_bufs, plain_bufs = (xp, z1p, z2p), (y1p, y2p, y3p)

    @pl.when(has_up == False)
    def _():
        raw_halo[...] = jnp.zeros(raw_halo.shape, BF16)
        for buf in pair_bufs + plain_bufs:
            buf[0] = jnp.zeros(buf.shape[1:], BF16)

    @pl.when(has_down == False)
    def _():
        for buf in plain_bufs:
            buf[buf.shape[0] - 1] = jnp.zeros(buf.shape[1:], BF16)

    @pl.when(is_left)
    def _():
        for buf in pair_bufs:
            buf[:, 0, 1] = jnp.zeros((buf.shape[0],) + buf.shape[3:], BF16)
        for buf in plain_bufs:
            buf[:, 0] = jnp.zeros((buf.shape[0],) + buf.shape[2:], BF16)

    @pl.when(is_right)
    def _():
        for buf in plain_bufs:
            buf[:, buf.shape[1] - 1] = jnp.zeros((buf.shape[0],) + buf.shape[2:], BF16)

    def raw_copy(h):
        slot = h % RAW
        return pltpu.make_async_copy(x_ref.at[:, h], raw.at[slot], raw_sem.at[slot])

    for h in range(7, 7 - RAW, -1):
        raw_copy(h).start()
    for copy in loads_d1:
        copy.start()
    barrier = pltpu.get_barrier_semaphore()

    def signal(row, col):
        pl.semaphore_signal(barrier, inc=1, device_id={"row": row, "col": col}, device_id_type=pl.DeviceIdType.MESH)

    signal(r, other)

    @pl.when(has_up)
    def _():
        signal(up, c)
        signal(up, other)

    @pl.when(has_down)
    def _():
        signal(down, c)
        signal(down, other)

    inner = has_up & has_down

    @pl.when(inner)
    def _():
        pl.semaphore_wait(barrier, 5)

    @pl.when(inner == False)
    def _():
        pl.semaphore_wait(barrier, 3)

    start(x_row)

    size = images * images

    def turn(src, index, row, b):
        at = pl.ds(b * images if isinstance(b, int) else pl.multiple_of(b * images, images), images)
        value = jnp.dot(perm[...], src[index + (slice(None), at)].reshape(size, c0), preferred_element_type=F32)
        xp[row, pl.ds(1 + b * (images // 2), images // 2)] = value.astype(BF16).reshape(images // 2, 2, images, c0)

    blocks = 2 * w1 // images

    def turn_rows(first, count):
        for h in range(first, first - count, -1):
            raw_copy(h).wait()
            for b in range(blocks):
                turn(raw, (h % RAW,), h + 1, b)
            if h >= RAW:
                raw_copy(h - RAW).start()

    def piece(taps, n_all, w, section, slot=None, fresh=True, bias=None, store=None):
        first, count = section
        for n0 in range(0, n_all, part):
            total = None
            for lhs, weight in taps:
                prod = jnp.dot(lhs(first, count), weight(n0), preferred_element_type=F32)
                total = prod if total is None else total + prod
            at = pl.ds((n0 // part) * w * images + first * images, count * images)
            if not fresh:
                total = total + acc[slot, at]
            if store is None:
                acc[slot, at] = total
            else:
                store(n0, jnp.maximum(total + bias[:, pl.ds(n0, part)], 0.0).astype(BF16), first, count)

    def pair_lhs(buf, row, kx):
        return lambda first, count: buf[row, pl.ds(first + (kx + 1) // 2, count), (kx + 1) % 2].reshape(count * images, buf.shape[4])

    def plain_lhs(buf, row, kx, k0=0, k=None):
        k = k or buf.shape[3]
        return lambda first, count: buf[row, pl.ds(first + kx, count), :, pl.ds(k0, k)].reshape(count * images, k)

    def plain_store(buf, h):
        def store(n0, value, first, count):
            buf[h + 1, pl.ds(1 + first, count), :, pl.ds(n0, part)] = value.reshape(count, images, part)
        return store

    def pair_store(buf, h):
        def store(n0, value, first, count):
            buf[h + 1, pl.ds(1 + first // 2, count // 2), :, :, pl.ds(n0, part)] = value.reshape(count // 2, 2, images, part)
        return store

    def down1(h, kys, section=(0, w1), final=True, **kw):
        taps = [(pair_lhs(xp, 2 * h + ky, kx), lambda n0, t=3 * ky + kx: block(place_d1(t), c0, n0)) for ky in kys for kx in TAPS]
        piece(taps, c1, w1, section, bias=bd1, store=plain_store(y1p, h) if final else None, **kw)

    def conv1(h, kys, section=(0, w1), final=True, proj=False, **kw):
        taps = [(plain_lhs(y1p, h + ky, kx), lambda n0, t=3 * ky + kx: block(place_c1(t), c1, n0)) for ky in kys for kx in TAPS]
        if proj:
            taps.append((pair_lhs(xp, 2 * h + 1, 1), lambda n0: block(place_d1(9), c0, n0)))
        piece(taps, c1, w1, section, bias=bc1, store=pair_store(z1p, h) if final else None, **kw)

    def down2(h, kys, section=(0, w2), final=True, **kw):
        taps = [(pair_lhs(z1p, 2 * h + ky, kx), lambda n0, t=3 * ky + kx: block(place_d2(t), c1, n0)) for ky in kys for kx in TAPS]
        piece(taps, c2, w2, section, bias=bd2, store=plain_store(y2p, h) if final else None, **kw)

    def conv2(h, kys, section=(0, w2), final=True, proj=False, **kw):
        taps = [(plain_lhs(y2p, h + ky, kx, kh * c1, c1), lambda n0, t=3 * ky + kx, kh=kh: block(place_c2(t, kh), c1, n0))
                for ky in kys for kx in TAPS for kh in range(2)]
        if proj:
            taps.append((pair_lhs(z1p, 2 * h + 1, 1), lambda n0: block(place_d2(9), c1, n0)))
        piece(taps, c2, w2, section, bias=bc2, store=pair_store(z2p, h) if final else None, **kw)

    m3 = w3 * images

    def group_dots(left, slot, into, fresh=False, n_range=None):
        for n0 in range(*(n_range or (0, c3)), part):
            at = pl.ds((n0 // part) * m3, m3)
            prod = jnp.dot(left, ring[slot, :, pl.ds(n0, part)], preferred_element_type=F32)
            acc[into, at] = prod if fresh else acc[into, at] + prod

    def z2_left(row, kx):
        return z2p[row, pl.ds((kx + 1) // 2, w3), (kx + 1) % 2].reshape(m3, c2)

    def down3(ky, g0):
        for kx in TAPS:
            slot = (g0 + kx + 8) % RING
            first_groups(g0 + kx).wait()
            group_dots(z2_left(ky, kx), slot, 0, fresh=g0 + kx == 0)
            conv3_first(g0 + kx)

    def conv3(first):
        def body(i, carry):
            slot = lax.rem(i + first + 8, RING)
            group_wait(slot)
            if first == 0:
                ky, kx, k0 = 1, i // 2, pl.multiple_of(lax.rem(i, 2) * c2, c2)
            else:
                ky, kx, k0 = 2 * (i // 3), lax.rem(i, 3), (first // 6 - 1) * c2
            left = y3p[ky, pl.ds(kx, w3), :, pl.ds(k0, c2)].reshape(m3, c2)
            group_dots(left, slot, 1)
            if first == 0:
                later = lax.rem(i + 4, 6)
                conv3_copy(6 * (later // 3) + lax.rem(later, 3), pl.multiple_of((i + 4) // 6 * c2, c2), slot).start()
            elif first == 6:
                @pl.when(i < 2)
                def _():
                    conv3_copy(7 + i, c2, slot).start()
            return carry
        lax.fori_loop(0, 6, body, 0)

    turn_rows(7, 3)
    start(x_col_b, x_diag)
    for copy in loads_c1:
        copy.start()
    turn_rows(4, 2)
    for copy in loads_d1:
        copy.wait()
    arrive(x_col_b)
    down1(3, TAPS)
    start(y1_ddown, y1_down)
    for copy in loads_d2:
        copy.start()
    turn_rows(2, 3)
    start(x_col_a)
    for copy in loads_c2:
        copy.start()
    arrive(x_col_a)
    down1(1, TAPS)
    down1(2, TAPS)
    start(y1_col_b)
    down1(0, TAPS[1:], slot=0, **MID)
    for copy in loads_c1:
        copy.wait()
    arrive(y1_col_b)
    conv1(2, TAPS, **PROJ)
    conv1(1, TAPS[1:], **PROJ, slot=1, **MID)
    conv1(3, TAPS[:2], **PROJ, slot=2, **MID)
    arrive(x_row, x_diag)
    for b in range(blocks):
        turn(raw_halo, (), 0, b)
    for i, section in enumerate(y1_parts):
        down1(0, TAPS[:1], section, slot=0, **END)
        start_with_diag(y1_ups[i], y1_dup, i)
    start(y1_col_a)
    arrive(y1_col_a)
    conv1(1, TAPS[:1], slot=1, **END)
    start(z1_cols[1])
    conv1(0, TAPS[1:], **PROJ, slot=0, **MID)
    for copy in loads_d2:
        copy.wait()
    arrive(z1_cols[1])
    down2(1, TAPS[:2], slot=1, **MID)
    for i, section in enumerate(z1_parts):
        arrive_with_diag(y1_ups[i], y1_dup, i)
        conv1(3, TAPS[2:], section, slot=2, **END)
        start(z1_rows[i])
    start(z1_cols[2], z1_diag)
    arrive(y1_down, y1_ddown)
    conv1(0, TAPS[:1], slot=0, **END)
    start(z1_cols[0])
    for g in range(2):
        first_groups(g).start()

    arrive(z1_cols[2])
    down2(1, TAPS[2:], slot=1, **END)
    start(y2_col_b, y2_ddown, y2_down)
    arrive(z1_cols[0])
    down2(0, TAPS[1:], slot=0, **MID)
    for copy in loads_c2:
        copy.wait()
    arrive(y2_col_b)
    conv2(1, TAPS[1:2], **PROJ, slot=1, **MID)
    conv2(0, TAPS[2:], **PROJ, slot=2, **MID)
    for g in (2, 3):
        first_groups(g).start()
    arrive(z1_diag)
    for i, section in enumerate(y2_parts):
        arrive(z1_rows[i])
        down2(0, TAPS[:1], section, slot=0, **END)
        start_with_diag(y2_ups[i], y2_dup, i)
    start(y2_col_a)
    first_groups(4).start()
    arrive(y2_col_a)
    conv2(1, TAPS[:1], slot=1, **END, **MID)
    conv2(0, TAPS[1:2], slot=2, **END, **MID)
    first_groups(5).start()
    for i, section in enumerate(z2_parts):
        arrive_with_diag(y2_ups[i], y2_dup, i)
        conv2(1, TAPS[2:], section, slot=1, **END)
        start(z2_rows[i])
    start(z2_cols[1], z2_diag)
    for g in (6, 7):
        first_groups(g).start()
    arrive(y2_down, y2_ddown)
    conv2(0, TAPS[:1], slot=2, **END)
    start(z2_cols[0])
    for g in (8, 9):
        first_groups(g).start()

    arrive(z2_cols[1])
    down3(2, 0)
    arrive(z2_cols[0])
    down3(1, 3)
    first_groups(6).wait()
    group_dots(z2_left(1, 1), (6 + 8) % RING, 1, fresh=True)
    conv3_first(6)
    arrive(*z2_rows, z2_diag)
    for g in range(7, 10):
        first_groups(g).wait()
    for half in range(2):
        for kx in TAPS:
            group_dots(z2_left(0, kx), (kx + 7 + 8) % RING, 0, n_range=(half * c2, half * c2 + c2))
        for n0 in range(half * c2, half * c2 + c2, part):
            total = acc[0, pl.ds((n0 // part) * m3, m3)] + bd3[:, pl.ds(n0, part)]
            y3p[1, pl.ds(1, w3), :, pl.ds(n0, part)] = jnp.maximum(total, 0.0).astype(BF16).reshape(w3, images, part)
        start(*y3_halves[half])
    for j in range(7, 10):
        conv3_first(j)
    arrive(y3_halves[0][0], y3_halves[1][0])
    conv3(0)
    arrive(*y3_halves[0][1:])
    conv3(6)
    arrive(*y3_halves[1][1:])
    conv3(12)
    for n0 in range(0, c3, part):
        total = acc[1, pl.ds((n0 // part) * m3, m3)] + bc3[:, pl.ds(n0, part)]
        out_v[:, :, pl.ds(n0, part)] = jnp.maximum(total, 0.0).astype(BF16).reshape(w3, images, part)
    put = pltpu.make_async_copy(out_v, out_ref, out_sem.at[0])
    put.start()
    under_conditions(copies)
    put.wait()


def solution(mesh):
    row_count = mesh.shape["row"]
    col_count = mesh.shape["col"]
    tile_spec = P("batch", "row", "col")

    def local_blocks(x_tile, *params):
        images, tile_h, tile_w, c0 = x_tile.shape
        weights, biases = [], []
        for stage in TAPS:
            w_down, b_down, w_conv, b_conv, w_proj = params[5 * stage:5 * stage + 5]
            weights += [w_down.reshape((9,) + w_down.shape[2:]), w_conv.reshape((9,) + w_conv.shape[2:]), w_proj]
            biases += [b_down.reshape(1, -1), b_conv.reshape(1, -1)]
        c1, c2, c3 = (weights[3 * stage].shape[2] for stage in TAPS)
        w1, w2, w3 = tile_w // 2, tile_w // 4, tile_w // 8
        any_spec = pl.BlockSpec(memory_space=pl.ANY)
        vmem_spec = pl.BlockSpec(memory_space=pltpu.VMEM)
        index = np.arange(images * images)
        perm = jnp.asarray(index[:, None] == (index % images * images + index // images)[None, :], BF16)
        copy_count = 39
        out = pl.pallas_call(
            lambda *refs: encoder_kernel(row_count, col_count, *refs),
            out_shape=jax.ShapeDtypeStruct((w3, images, c3), BF16),
            in_specs=[any_spec] * 10 + [vmem_spec] * 7,
            out_specs=any_spec,
            scratch_shapes=[
                pltpu.VMEM((tile_h + 1, w1 + 1, 2, images, c0), BF16),
                pltpu.VMEM((6, w1 + 2, images, c1), BF16),
                pltpu.VMEM((5, w2 + 1, 2, images, c1), BF16),
                pltpu.VMEM((4, w2 + 2, images, c2), BF16),
                pltpu.VMEM((3, w3 + 1, 2, images, c2), BF16),
                pltpu.VMEM((3, w3 + 2, images, c3), BF16),
                pltpu.VMEM((RING, c2, c3), BF16),
                pltpu.VMEM((3, w1 * images, c1), F32),
                pltpu.VMEM((w3, images, c3), BF16),
                pltpu.VMEM((RAW, images, tile_w, c0), BF16),
                pltpu.VMEM((images, tile_w, c0), BF16),
                pltpu.SemaphoreType.DMA(TAPS[1:2]),
                pltpu.SemaphoreType.DMA((RAW,)),
                pltpu.SemaphoreType.DMA((19,)),
                pltpu.SemaphoreType.DMA((28,)),
                pltpu.SemaphoreType.DMA((RING,)),
                pltpu.SemaphoreType.DMA((copy_count,)),
                pltpu.SemaphoreType.DMA((copy_count,)),
            ],
            compiler_params=pltpu.CompilerParams(collective_id=0, has_side_effects=True, vmem_limit_bytes=67043328),
            name="encoder",
        )(x_tile, *weights, *biases, perm)
        return out.transpose(1, 0, 2).reshape(images, 1, w3, c3)

    return jax.shard_map(local_blocks, mesh=mesh, in_specs=(tile_spec,) + (P(),) * 15, out_specs=tile_spec, check_vma=False)
```

time: 258 us -> 97.8 us (0.38); the launches traced: 254 us -> 97.6 us
  Pallas kernels: 0 us -> 95.5 us
  waiting for transfers between devices: 80.6 us -> 0 us
  matrix products: 78.8 us -> 0 us
  starting transfers between devices: 54.9 us -> 0 us
  local copies, waits for them, and re-layouts: 37.9 us -> 2.13 us
    pallas_call x0 -> x1, Pallas kernels: none -> 95.5 us  [local_blocks(): pl.pallas_call(lambda *refs: encoder_kernel(row_count, col_count, *refs),...]
    ppermute x18 -> x0, waiting for transfers between devices: 80.6 us -> none  [the longest x12 78.3 us: from_lower(): lax.ppermute(edge_part, axis_name, [(dev_index, dev_index + 1) for dev_in...]
    conv_general_dilated x6 -> x0, matrix products: 76.5 us -> none  [conv_valid(): lax.conv_general_dilated(act_in, weight, (stride, stride), 'VALID', dimen...]
    ppermute x18 -> x0, starting transfers between devices: 54.9 us -> none  [the longest x6 33.4 us: from_upper(): lax.ppermute(edge_part, axis_name, [(dev_index + 1, dev_index) for dev_in...]
    slice x7 -> x0, local copies, waits for them, and re-layouts: 30.3 us -> none  [the longest x1 27.8 us: basic_block(): z_prev[:, ::2, ::2]]
    concatenate x1 -> x0, local copies, waits for them, and re-layouts: 4.75 us -> none  [pad_lower(): tall_tile = jnp.concatenate([top_row, tile_in], axis=1)]
  transfers between devices with their start and end apart: 18 -> 0, of which waited for: 12 -> 0; matrix products, arithmetic and copies ran while one was open for 12% -> 0% of each run, Pallas kernels for 0% -> 0%
where the time goes in v2:
time: 97.8 us; the launch traced here: 97.6 us
  Pallas kernels  95.5 us (98%)
  local copies, waits for them, and re-layouts  2.13 us (2%)
    pallas_call x1, Pallas kernels, local_blocks(): pl.pallas_call(lambda *refs: encoder_kernel(row_count, col_count, *refs),...  95.5 us
    reshape x1, local copies, waits for them, and re-layouts, local_blocks(): return out.transpose(1, 0, 2).reshape(images, 1, w3, c3)  2.13 us

profile of v2, /device:TPU:97, one launch (start us, length us, event | category | flops | bytes accessed | tf_op | source)
XLA Modules:
  0.0 97.6 jit_solution(8514584637970945668)
XLA Ops:
  0.0 95.5 %encoder.1 = bf16[8,16,2048]{2,1,0:T(8,128)(2,1)} custom-call(bf16[16,8,64,256]{3,2,1,0:T(8,128)(2,1)} %refs_0_.1, bf16[9,256,512]{2,1,0:T(8,128)(2,1)} %bitcast.19, bf16[9,512,512]{2,1,0:T(8,128)(2,1)} %bitcast.18, bf16[256,512]{1,0:T(8,128)(2,1)} %refs_3_.1, bf16[9,512,1024]{2,1,0:T(8,128)(2,1)} %bitcast.17, bf16[9,1024,1024]{2,1,0:T(8,128)(2,1)} %bitcast.16, ...), custom_call_target="tpu_custom_call" | custom-call | tf_op jit(solution)/shard_map/encoder/pallas_call | solution.py:509
  95.5 2.1 %copy.18 = bf16[16,1,8,2048]{3,2,1,0:T(8,128)(2,1)} copy(bf16[16,1,8,2048]{3,0,2,1:T(8,128)(2,1)} %bitcast.20) | data formatting | bytes 1048576 | tf_op jit(solution)/shard_map/reshape | solution.py:537

commit v3 on v2

--- a/solution.py
+++ b/solution.py
@@ -24,7 +24,7 @@
     has_down = r < rows - 1
     images = x_ref.shape[0]
     part = acc.shape[2]
-    c0, c1, c2, c3 = x_ref.shape[3], wd1.shape[2], wd2.shape[2], wd3.shape[2]
+    c0, c1, c2, c3 = x_ref.shape[4], wd1.shape[2], wd2.shape[2], wd3.shape[2]
 
     def place_c1(t):
         if t == 8:
@@ -96,13 +96,15 @@
 
     w1, w2, w3 = y1p.shape[1] - 2, y2p.shape[1] - 2, y3p.shape[1] - 2
 
-    def parts(w, a):
-        return (0, a), (a, w - a)
-
-    y1_parts = parts(w1, w2 + 3)
-    z1_parts = parts(w1, w2 + 2)
-    y2_parts = parts(w2, w3 + 1)
-    z2_parts = parts(w2, w3)
+    def parts(*ends):
+        return [(first, end - first) for first, end in zip((0,) + ends, ends)]
+
+    z2_ends = (3 * w3 // 4, 5 * w3 // 4, w2)
+    y2_ends = [min(end + 1, w2) for end in z2_ends]
+    z1_ends = [2 * end for end in y2_ends]
+    y1_ends = [min(end + 1, w1) for end in z1_ends]
+    z2_parts, y2_parts, z1_parts, y1_parts = parts(*z2_ends), parts(*y2_ends), parts(*z1_ends), parts(*y1_ends)
+    x_parts = parts(*[-(-2 * end // images) for end in y1_ends])
 
     def pair_rows(buf, sections):
         n = buf.shape[0]
@@ -151,7 +153,7 @@
         at = (pl.ds(0, images), pl.ds(k0, k))
         return halo(buf.at[(pl.ds(first, count), src_col) + at], buf.at[(pl.ds(first, count), dst_col) + at], r, other, None, None)
 
-    x_row = halo(x_ref.at[:, 7], raw_halo, down, c, has_down, has_up)
+    x_rows = [halo(x_ref.at[:, 7, pl.ds(first, count)], raw_halo.at[:, pl.ds(first, count)], down, c, has_down, has_up) for first, count in x_parts]
     x_diag = pair_diag(xp)
     x_col_b, x_col_a = pair_col(xp, 6, 3), pair_col(xp, 1, 5)
     y1_down, y1_ups = plain_down(y1p), plain_ups(y1p, y1_parts)
@@ -169,6 +171,8 @@
         y3_halves.append((plain_col(y3p, 1, 1, k0, c2), plain_diag(y3p, True, k0, c2), plain_diag(y3p, False, k0, c2),
                           plain_down(y3p, k0, c2), plain_ups(y3p, ((0, w3),), k0, c2)[0]))
 
+    assert len(copies) == send_sem.shape[0]
+
     def under_conditions(items):
         groups = {}
         for condition, action in items:
@@ -188,11 +192,21 @@
     def arrive(*ops):
         under_conditions([(recv_if, copy.wait_recv) for copy, _, recv_if in ops])
 
-    def start_with_diag(row, diag, last):
-        under_conditions([(has_up, row[0].start), (up_left if last else up_right, diag[0].start)])
-
-    def arrive_with_diag(row, diag, last):
-        under_conditions([(has_down, row[0].wait_recv), (down_left if last else down_right, diag[0].wait_recv)])
+    def start_part(rows, diag, i):
+        items = [(has_up, rows[i][0].start)]
+        if i == 0:
+            items.append((up_right, diag[0].start))
+        if i == len(rows) - 1:
+            items.append((up_left, diag[0].start))
+        under_conditions(items)
+
+    def arrive_part(rows, diag, i):
+        items = [(has_down, rows[i][0].wait_recv)]
+        if i == 0:
+            items.append((down_right, diag[0].wait_recv))
+        if i == len(rows) - 1:
+            items.append((down_left, diag[0].wait_recv))
+        under_conditions(items)
 
     pair_bufs, plain_bufs = (xp, z1p, z2p), (y1p, y2p, y3p)
 
@@ -254,13 +268,12 @@
     def _():
         pl.semaphore_wait(barrier, 3)
 
-    start(x_row)
+    start(*x_rows)
 
     size = images * images
 
     def turn(src, index, row, b):
-        at = pl.ds(b * images if isinstance(b, int) else pl.multiple_of(b * images, images), images)
-        value = jnp.dot(perm[...], src[index + (slice(None), at)].reshape(size, c0), preferred_element_type=F32)
+        value = jnp.dot(perm[...], src[index + (slice(None), b)].reshape(size, c0), preferred_element_type=F32)
         xp[row, pl.ds(1 + b * (images // 2), images // 2)] = value.astype(BF16).reshape(images // 2, 2, images, c0)
 
     blocks = 2 * w1 // images
@@ -391,12 +404,13 @@
     conv1(2, TAPS, **PROJ)
     conv1(1, TAPS[1:], **PROJ, slot=1, **MID)
     conv1(3, TAPS[:2], **PROJ, slot=2, **MID)
-    arrive(x_row, x_diag)
-    for b in range(blocks):
-        turn(raw_halo, (), 0, b)
+    arrive(x_diag)
     for i, section in enumerate(y1_parts):
+        arrive(x_rows[i])
+        for b in range(x_parts[i][0], sum(x_parts[i])):
+            turn(raw_halo, (), 0, b)
         down1(0, TAPS[:1], section, slot=0, **END)
-        start_with_diag(y1_ups[i], y1_dup, i)
+        start_part(y1_ups, y1_dup, i)
     start(y1_col_a)
     arrive(y1_col_a)
     conv1(1, TAPS[:1], slot=1, **END)
@@ -407,7 +421,7 @@
     arrive(z1_cols[1])
     down2(1, TAPS[:2], slot=1, **MID)
     for i, section in enumerate(z1_parts):
-        arrive_with_diag(y1_ups[i], y1_dup, i)
+        arrive_part(y1_ups, y1_dup, i)
         conv1(3, TAPS[2:], section, slot=2, **END)
         start(z1_rows[i])
     start(z1_cols[2], z1_diag)
@@ -433,7 +447,7 @@
     for i, section in enumerate(y2_parts):
         arrive(z1_rows[i])
         down2(0, TAPS[:1], section, slot=0, **END)
-        start_with_diag(y2_ups[i], y2_dup, i)
+        start_part(y2_ups, y2_dup, i)
     start(y2_col_a)
     first_groups(4).start()
     arrive(y2_col_a)
@@ -441,7 +455,7 @@
     conv2(0, TAPS[1:2], slot=2, **END, **MID)
     first_groups(5).start()
     for i, section in enumerate(z2_parts):
-        arrive_with_diag(y2_ups[i], y2_dup, i)
+        arrive_part(y2_ups, y2_dup, i)
         conv2(1, TAPS[2:], section, slot=1, **END)
         start(z2_rows[i])
     start(z2_cols[1], z2_diag)
@@ -505,7 +519,7 @@
         vmem_spec = pl.BlockSpec(memory_space=pltpu.VMEM)
         index = np.arange(images * images)
         perm = jnp.asarray(index[:, None] == (index % images * images + index // images)[None, :], BF16)
-        copy_count = 39
+        copy_count = 45
         out = pl.pallas_call(
             lambda *refs: encoder_kernel(row_count, col_count, *refs),
             out_shape=jax.ShapeDtypeStruct((w3, images, c3), BF16),
@@ -521,8 +535,8 @@
                 pltpu.VMEM((RING, c2, c3), BF16),
                 pltpu.VMEM((3, w1 * images, c1), F32),
                 pltpu.VMEM((w3, images, c3), BF16),
-                pltpu.VMEM((RAW, images, tile_w, c0), BF16),
-                pltpu.VMEM((images, tile_w, c0), BF16),
+                pltpu.VMEM((RAW, images, tile_w // images, images, c0), BF16),
+                pltpu.VMEM((images, tile_w // images, images, c0), BF16),
                 pltpu.SemaphoreType.DMA(TAPS[1:2]),
                 pltpu.SemaphoreType.DMA((RAW,)),
                 pltpu.SemaphoreType.DMA((19,)),
@@ -533,7 +547,7 @@
             ],
             compiler_params=pltpu.CompilerParams(collective_id=0, has_side_effects=True, vmem_limit_bytes=67043328),
             name="encoder",
-        )(x_tile, *weights, *biases, perm)
+        )(x_tile.reshape(images, tile_h, tile_w // images, images, c0), *weights, *biases, perm)
         return out.transpose(1, 0, 2).reshape(images, 1, w3, c3)
 
     return jax.shard_map(local_blocks, mesh=mesh, in_specs=(tile_spec,) + (P(),) * 15, out_specs=tile_spec, check_vma=False)

time: 97.8 us -> 97.1 us (level)
  no operation moved by 1% of the time
where the time goes in v3:
time: 97.1 us; the launch traced here: 96.9 us
  Pallas kernels  94.7 us (98%)
  local copies, waits for them, and re-layouts  2.13 us (2%)
    pallas_call x1, Pallas kernels, local_blocks(): pl.pallas_call(lambda *refs: encoder_kernel(row_count, col_count, *refs),...  94.7 us
    reshape x1, local copies, waits for them, and re-layouts, local_blocks(): return out.transpose(1, 0, 2).reshape(images, 1, w3, c3)  2.13 us

profile of v3, /device:TPU:97, one launch (start us, length us, event | category | flops | bytes accessed | tf_op | source)
XLA Modules:
  0.0 96.9 jit_solution(13686182916988753930)
XLA Ops:
  0.0 94.7 %encoder.1 = bf16[8,16,2048]{2,1,0:T(8,128)(2,1)} custom-call(bf16[16,8,4,16,256]{4,3,2,1,0:T(8,128)(2,1)} %bitcast.20, bf16[9,256,512]{2,1,0:T(8,128)(2,1)} %bitcast.21, bf16[9,512,512]{2,1,0:T(8,128)(2,1)} %bitcast.19, bf16[256,512]{1,0:T(8,128)(2,1)} %refs_3_.1, bf16[9,512,1024]{2,1,0:T(8,128)(2,1)} %bitcast.18, bf16[9,1024,1024]{2,1,0:T(8,128)(2,1)} %bitcast.17, ...), custom_call_target="tpu_custom_call" | custom-call | tf_op jit(solution)/shard_map/encoder/pallas_call | solution.py:523
  94.8 2.1 %copy.18 = bf16[16,1,8,2048]{3,2,1,0:T(8,128)(2,1)} copy(bf16[16,1,8,2048]{3,0,2,1:T(8,128)(2,1)} %bitcast.22) | data formatting | bytes 1048576 | tf_op jit(solution)/shard_map/reshape | solution.py:551

commit v4 on v3

--- a/solution.py
+++ b/solution.py
@@ -461,14 +461,14 @@
     start(z2_cols[1], z2_diag)
     for g in (6, 7):
         first_groups(g).start()
+    arrive(z2_cols[1])
+    down3(2, 0)
     arrive(y2_down, y2_ddown)
     conv2(0, TAPS[:1], slot=2, **END)
     start(z2_cols[0])
     for g in (8, 9):
         first_groups(g).start()
 
-    arrive(z2_cols[1])
-    down3(2, 0)
     arrive(z2_cols[0])
     down3(1, 3)
     first_groups(6).wait()

time: 97.1 us -> 97 us (level)
    pallas_call x1, Pallas kernels: 94.7 us -> 93.8 us  [local_blocks(): pl.pallas_call(lambda *refs: encoder_kernel(row_count, col_count, *refs),...]
where the time goes in v4:
time: 97 us; the launch traced here: 95.9 us
  Pallas kernels  93.8 us (97%)
  local copies, waits for them, and re-layouts  2.13 us (2%)
    pallas_call x1, Pallas kernels, local_blocks(): pl.pallas_call(lambda *refs: encoder_kernel(row_count, col_count, *refs),...  93.8 us
    reshape x1, local copies, waits for them, and re-layouts, local_blocks(): return out.transpose(1, 0, 2).reshape(images, 1, w3, c3)  2.13 us

profile of v4, /device:TPU:97, one launch (start us, length us, event | category | flops | bytes accessed | tf_op | source)
XLA Modules:
  0.0 95.9 jit_solution(10769049416693831887)
XLA Ops:
  0.0 93.8 %encoder.1 = bf16[8,16,2048]{2,1,0:T(8,128)(2,1)} custom-call(bf16[16,8,4,16,256]{4,3,2,1,0:T(8,128)(2,1)} %bitcast.20, bf16[9,256,512]{2,1,0:T(8,128)(2,1)} %bitcast.21, bf16[9,512,512]{2,1,0:T(8,128)(2,1)} %bitcast.19, bf16[256,512]{1,0:T(8,128)(2,1)} %refs_3_.1, bf16[9,512,1024]{2,1,0:T(8,128)(2,1)} %bitcast.18, bf16[9,1024,1024]{2,1,0:T(8,128)(2,1)} %bitcast.17, ...), custom_call_target="tpu_custom_call" | custom-call | tf_op jit(solution)/shard_map/encoder/pallas_call | solution.py:523
  93.8 2.1 %copy.18 = bf16[16,1,8,2048]{3,2,1,0:T(8,128)(2,1)} copy(bf16[16,1,8,2048]{3,0,2,1:T(8,128)(2,1)} %bitcast.22) | data formatting | bytes 1048576 | tf_op jit(solution)/shard_map/reshape | solution.py:551

commit v5 on v4

--- a/solution.py
+++ b/solution.py
@@ -401,11 +401,10 @@
     for copy in loads_c1:
         copy.wait()
     arrive(y1_col_b)
-    conv1(2, TAPS, **PROJ)
-    conv1(1, TAPS[1:], **PROJ, slot=1, **MID)
-    conv1(3, TAPS[:2], **PROJ, slot=2, **MID)
     arrive(x_diag)
+    fill = (lambda: conv1(2, TAPS, **PROJ), lambda: conv1(1, TAPS[1:], **PROJ, slot=1, **MID), lambda: conv1(3, TAPS[:2], **PROJ, slot=2, **MID))
     for i, section in enumerate(y1_parts):
+        fill[i]()
         arrive(x_rows[i])
         for b in range(x_parts[i][0], sum(x_parts[i])):
             turn(raw_halo, (), 0, b)

time: 97 us -> 96.8 us (level)
  no operation moved by 1% of the time
where the time goes in v5:
time: 96.8 us; the launch traced here: 96.6 us
  Pallas kernels  94.4 us (98%)
  local copies, waits for them, and re-layouts  2.13 us (2%)
    pallas_call x1, Pallas kernels, local_blocks(): pl.pallas_call(lambda *refs: encoder_kernel(row_count, col_count, *refs),...  94.4 us
    reshape x1, local copies, waits for them, and re-layouts, local_blocks(): return out.transpose(1, 0, 2).reshape(images, 1, w3, c3)  2.13 us

profile of v5, /device:TPU:97, one launch (start us, length us, event | category | flops | bytes accessed | tf_op | source)
XLA Modules:
  0.0 96.6 jit_solution(8941130472928795085)
XLA Ops:
  0.0 94.4 %encoder.1 = bf16[8,16,2048]{2,1,0:T(8,128)(2,1)} custom-call(bf16[16,8,4,16,256]{4,3,2,1,0:T(8,128)(2,1)} %bitcast.20, bf16[9,256,512]{2,1,0:T(8,128)(2,1)} %bitcast.21, bf16[9,512,512]{2,1,0:T(8,128)(2,1)} %bitcast.19, bf16[256,512]{1,0:T(8,128)(2,1)} %refs_3_.1, bf16[9,512,1024]{2,1,0:T(8,128)(2,1)} %bitcast.18, bf16[9,1024,1024]{2,1,0:T(8,128)(2,1)} %bitcast.17, ...), custom_call_target="tpu_custom_call" | custom-call | tf_op jit(solution)/shard_map/encoder/pallas_call | solution.py:522
  94.4 2.1 %copy.18 = bf16[16,1,8,2048]{3,2,1,0:T(8,128)(2,1)} copy(bf16[16,1,8,2048]{3,0,2,1:T(8,128)(2,1)} %bitcast.22) | data formatting | bytes 1048576 | tf_op jit(solution)/shard_map/reshape | solution.py:550
